TPU v7x, 512 devices: a whole 4x4x16 slice. The times are simulated.
512 devices in a mesh: rep: 16 (over y, z_lo), zero: 32 (over z_hi, x, core).
Axes of the slice: x: 4, y: 4, z: 16 (z_hi: 4, z_lo: 4; z = z_hi * 4 + z_lo), core: 2. Of those that a mesh axis runs over, the one named last changes fastest.
Arguments:
- pre_norm: bfloat16 [8192, 8192], P(('rep', 'zero')), may hold values from -6 to 6
- upstream: bfloat16 [8192, 8192], P(('rep', 'zero')), may hold values from -20 to 20
- norm_gain: float32 [8192], replicated, may hold values from 0.1 to 1.9
- saved_mean: float32 [8192], replicated, may hold values from -4 to 4
- inv_std: float32 [8192], replicated, may hold values from 0.5 to 1.5
- features: bfloat16 [401408, 512], P(('rep', 'zero')), may hold values from -24 to 24
- out_grads: bfloat16 [401408, 2048], P(('rep', 'zero')), may hold values from -24 to 24
Outputs:
- input_grad: bfloat16 [8192, 8192], P(('rep', 'zero'))
- gain_grad: float32 [8192], replicated
- bias_grad: float32 [8192], replicated
- weight_grad: float32 [512, 2048], P('zero')
All inputs are finite; a program needn't handle non-finite values.
Results may differ from a plain program's by a relative error of at most 0.001.
Values sent between devices are 32-bit elements; how exact they have to be, the bound alone decides.
A program may use at most 64 MiB of HBM per device.

v0:
```python
import jax
import jax.numpy as jnp
from jax import lax
from jax.sharding import Mesh
from jax.sharding import PartitionSpec as P

ZERO = ("zero_0", "zero_1", "zero_2")
REP_ZERO = ("rep", "zero_0", "zero_1", "zero_2")


def gathered_total(x, axis):
    parts = lax.all_gather(x, axis)
    return parts.sum(axis=0)


def sent_to_all(x, axis):
    copies = jnp.broadcast_to(x, (lax.axis_size(axis), *x.shape))
    return lax.all_to_all(copies, axis, split_axis=0, concat_axis=0, tiled=True)


def taken_together(x, axis):
    everything = sent_to_all(x, axis)
    return jnp.sum(everything, axis=0)


def split_up(x, dim, length):
    shape = x.shape
    parts = x.reshape(*shape[:dim], length, shape[dim] // length, *shape[dim + 1 :])
    return jnp.moveaxis(parts, dim, 0)


def summed_rows(x, chips, core, dim):
    sizes = (lax.axis_size(chips), lax.axis_size(core))
    parts = split_up(x, dim, sizes[0] * sizes[1])
    inside = parts.shape[1:]
    parts = parts.reshape(*sizes, *inside).swapaxes(0, 1).reshape(-1, *inside)
    parts = lax.psum_scatter(parts, core, scatter_dimension=0, tiled=True)
    return lax.psum_scatter(parts, chips, scatter_dimension=0, tiled=True)[0]


def per_device(pre_norm, upstream, norm_gain, saved_mean, inv_std, features, out_grads):
    num_rep = lax.axis_size("rep")
    num_zero = lax.axis_size(ZERO)
    all_images = pre_norm.shape[0] * num_rep * num_zero
    normed = (pre_norm.astype(jnp.float32) - saved_mean) * inv_std
    grads32 = upstream.astype(jnp.float32)
    local_sums = jnp.stack((jnp.sum(grads32, axis=0), jnp.sum(grads32 * normed, axis=0)))
    group_sums = gathered_total(local_sums, ZERO)
    stacked_sums = taken_together(group_sums, "rep")
    bias_grad = stacked_sums[0] / all_images
    gain_grad = stacked_sums[1] / all_images
    input_grad = (norm_gain * inv_std * (grads32 - bias_grad - normed * gain_grad)).astype(
        jnp.bfloat16
    )
    partial_grad = lax.dot_general(
        features, out_grads, (((0,), (0,)), ((), ())), preferred_element_type=jnp.float32
    )
    owner_rows = summed_rows(partial_grad, ("zero_0", "zero_1"), "zero_2", 0)
    owner_total = taken_together(owner_rows, "rep")
    weight_grad = owner_total / all_images
    return (input_grad, gain_grad, bias_grad, weight_grad)


def solution(mesh):
    finer = Mesh(
        mesh.devices.reshape(mesh.shape["rep"], 4, 4, 2), ("rep", "zero_0", "zero_1", "zero_2")
    )
    placed = (
        P(REP_ZERO, None),
        P(REP_ZERO, None),
        P(),
        P(),
        P(),
        P(REP_ZERO, None),
        P(REP_ZERO, None),
    )
    return jax.shard_map(
        per_device,
        mesh=finer,
        in_specs=placed,
        out_specs=(P(REP_ZERO, None), P(), P(), P(ZERO, None)),
        check_vma=False,
    )
```

profile of v0, /device:TPU:4, one launch (start us, length us, event | category | flops | bytes accessed | tf_op | source)
XLA Modules:
  0.0 257.2 jit_solution(16286723844778433641)
XLA Ops:
  8.0 0.0 copy-start
  8.0 0.0 reduce-scatter.3.cloned.1.call-start
  8.1 1.9 copy-done
  9.9 3.5 %fusion.4 = f32[512,2048]{1,0:T(8,128)S(1)} fusion(bf16[784,512]{1,0:T(8,128)(2,1)} %param.12, bf16[784,2048]{1,0:T(8,128)(2,1)S(1)} %copy-done), kind=kOutput, calls=%fused_computation.12 | convolution fusion | flops 1644167168 | bytes 8208384 | tf_op jit(solution)/shard_map/dot_general | solution.py:55
  13.4 2.2 copy.15
  15.6 0.0 copy-start.1
  15.6 0.0 copy-start.2
  15.6 0.0 copy-start.3
  15.6 0.0 reduce-scatter.3.cloned.1.call-update
  15.7 0.0 all-gather.4.cloned.1.call-start
  15.7 0.9 copy-done.1
  16.6 0.0 copy-done.2
  16.6 0.0 copy-done.3
  16.6 1.2 convert_reduce_fusion
  17.8 0.7 maximum_bitcast_fusion
  18.5 0.0 all-gather.4.cloned.1.call-update
  18.5 0.0 reduce-scatter.5.cloned.1.call-start
  18.5 24.3 %reduce-scatter.3.cloned.1.call-done = f32[16,16,2048]{2,1,0:T(8,128)} async-done(((f32[32,16,2048]{2,1,0:T(8,128)}), f32[16,16,2048]{2,1,0:T(8,128)}) %reduce-scatter.3.cloned.1.call-update) | async-done | bytes 2097168 | tf_op jit(solution)/shard_map/reduce_scatter | solution.py:37
  42.8 0.0 reduce-scatter.5.cloned.1.call-update
  42.9 63.9 %all-gather.4.cloned.1.call-done = f32[32,2,8192]{2,1,0:T(2,128)} async-done(((f32[1,2,8192]{2,1,0:T(2,128)}), f32[32,2,8192]{2,1,0:T(2,128)}) %all-gather.4.cloned.1.call-update) | async-done | bytes 2097168 | tf_op jit(solution)/shard_map/all_gather | solution.py:12
  106.8 2.9 %reduce_sum.47 = f32[2,8192]{1,0:T(2,128)} reduce(f32[32,2,8192]{2,1,0:T(2,128)} %all-gather.4.cloned.1.call-done, f32[]{:T(128)} %constant.6.clone.1), dimensions={0}, to_apply=%region_2.0 | reduce | flops 507904 | bytes 2162692 | tf_op jit(solution)/shard_map/reduce_sum | solution.py:13
  109.7 1.2 broadcast_in_dim.4
  111.0 46.8 %all_to_all.10 = f32[16,2,8192]{2,1,0:T(2,128)} all-to-all(f32[16,2,8192]{2,1,0:T(2,128)S(1)} %broadcast_in_dim.4), channel_id=1, replica_groups=mesh['rep'=16,'zero_0'=4,'zero_1'=4,'zero_2'=2] {'rep'}, dimensions={0} | all-to-all | bytes 2097152 | tf_op jit(solution)/shard_map/all_to_all | solution.py:18
  157.7 30.9 %reduce-scatter.5.cloned.1.call-done = f32[1,16,2048]{2,1,0:T(8,128)} async-done(((f32[16,16,2048]{2,1,0:T(8,128)}), f32[1,16,2048]{2,1,0:T(8,128)}) %reduce-scatter.5.cloned.1.call-update) | async-done | bytes 131088 | tf_op jit(solution)/shard_map/reduce_scatter | solution.py:38
  188.6 2.5 broadcast_in_dim.5
  191.1 6.6 %all-to-all-start.1 = ((f32[16,16,2048]{2,1,0:T(8,128)}), f32[16,16,2048]{2,1,0:T(8,128)}, u32[]{:S(2)}, u32[]{:S(2)}) async-start(f32[16,16,2048]{2,1,0:T(8,128)} %broadcast_in_dim.5), calls=%async_computation.3 | async-start | bytes 4194304 | tf_op jit(solution)/shard_map/all_to_all | solution.py:18
  197.7 1.4 mul.32
  199.1 2.2 reduce_sum.48
  201.3 1.0 slice_multiply_fusion.1
  202.2 0.0 copy-start.4
  202.3 0.0 copy-start.5
  202.3 0.6 copy-done.4
  202.9 0.0 copy-done.5
  202.9 1.8 fusion.3
  204.7 42.7 %all-to-all-done.1 = f32[16,16,2048]{2,1,0:T(8,128)} async-done(((f32[16,16,2048]{2,1,0:T(8,128)}), f32[16,16,2048]{2,1,0:T(8,128)}, u32[]{:S(2)}, u32[]{:S(2)}) %all-to-all-start.1) | async-done | bytes 2097184 | tf_op jit(solution)/shard_map/all_to_all | solution.py:18
  247.4 1.7 reduce_sum.49
  249.1 0.7 broadcast_multiply_fusion
Async XLA Ops:
  8.0 1.9 copy-start
  8.0 34.8 %reduce-scatter.3.cloned.1.call-start = ((), (), s32[]{:S(2)}) async-start(), calls=%async_computation.4 | async-start | bytes 6291456 | tf_op jit(solution)/shard_map/reduce_scatter | solution.py:37
  15.6 0.9 copy-start.1
  15.6 1.0 copy-start.2
  15.6 1.0 copy-start.3
  15.7 91.2 %all-gather.4.cloned.1.call-start = ((), (), s32[]{:S(2)}) async-start(), calls=%async_computation.6 | async-start | bytes 2162688 | tf_op jit(solution)/shard_map/all_gather | solution.py:12
  18.5 170.1 %reduce-scatter.5.cloned.1.call-start = ((), (), s32[]{:S(2)}) async-start(), calls=%async_computation.5 | async-start | bytes 2228224 | tf_op jit(solution)/shard_map/reduce_scatter | solution.py:38
  191.1 56.3 %all-to-all-start.1 = ((f32[16,16,2048]{2,1,0:T(8,128)}), f32[16,16,2048]{2,1,0:T(8,128)}, u32[]{:S(2)}, u32[]{:S(2)}) async-start(f32[16,16,2048]{2,1,0:T(8,128)} %broadcast_in_dim.5), calls=%async_computation.3 | async-start | bytes 4194304 | tf_op jit(solution)/shard_map/all_to_all | solution.py:18
  202.2 0.6 copy-start.4
  202.3 0.6 copy-start.5
Sparse Core Ops, SparseCore 0:
  15.8 27.0 reduce-scatter.2
  47.0 141.5 reduce-scatter.4
Sparse Core Ops, SparseCore 1:
  19.8 86.9 all-gather.3
where the time goes:
time: 258 us; the launch traced here: 257 us
  waiting for transfers between devices  162 us (63%)
  blocking collectives  46.8 us (18%)
  between operations  15.5 us (6%)
  other arithmetic  13.5 us (5%)
  local copies, waits for them, and re-layouts  9.28 us (4%)
  starting transfers between devices  6.71 us (3%)
  matrix products  3.51 us (1%)
    all_gather x1, waiting for transfers between devices, gathered_total(): parts = lax.all_gather(x, axis)  63.9 us
    all_to_all x1, blocking collectives, sent_to_all(): return lax.all_to_all(copies, axis, split_axis=0, concat_axis=0, tiled=True)  46.8 us
    all_to_all x1, waiting for transfers between devices, sent_to_all(): return lax.all_to_all(copies, axis, split_axis=0, concat_axis=0, tiled=True)  42.7 us
    reduce_scatter x1, waiting for transfers between devices, summed_rows(): return lax.psum_scatter(parts, chips, scatter_dimension=0, tiled=True)[0]  30.9 us
    reduce_scatter x1, waiting for transfers between devices, summed_rows(): parts = lax.psum_scatter(parts, core, scatter_dimension=0, tiled=True)  24.3 us
    all_to_all x1, starting transfers between devices, sent_to_all(): return lax.all_to_all(copies, axis, split_axis=0, concat_axis=0, tiled=True)  6.58 us
  transfers between devices with their start and end apart: 4, of which 4 were waited for; matrix products, arithmetic and copies ran while one was open for 5% of the time, Pallas kernels for 0%

commit v1 on v0

v1 whole, which is shorter than its diff:
```python
import functools

import jax
import jax.numpy as jnp
from jax import lax
from jax.experimental import pallas as pl
from jax.experimental.pallas import tpu as pltpu
from jax.sharding import PartitionSpec as P

MESH = pl.DeviceIdType.MESH
F = 8192
ROWS = 784
CIN = 512
COUT = 2048
IMAGES = 8192
NX, NY, NZL, NZH = 4, 4, 4, 4
NZ = NZL * NZH
W = 256
F_CORE, F_X, F_Y = F // 2, F // 8, F // 32


def mul(v, m):
    return pl.multiple_of(v, m)


class Copies:
    def __init__(self, send, recv):
        self.send, self.recv, self.n, self.all = send, recv, 0, []

    def make(self, src, dst, device):
        i = self.n
        self.n += 1
        copy = pltpu.make_async_remote_copy(
            src_ref=src,
            dst_ref=dst,
            send_sem=self.send.at[i],
            recv_sem=self.recv.at[i],
            device_id=device,
            device_id_type=MESH,
        )
        copy.start()
        self.all.append(copy)
        return copy


class Ring4:
    def __init__(self, copies, src, bufs, plus, minus):
        self.c, self.src, self.bufs, self.plus, self.minus = copies, src, bufs, plus, minus

    def send2(self):
        self.two_a = self.c.make(self.src(2, 0), self.bufs.at[0], self.plus)
        self.two_b = self.c.make(self.src(2, 1), self.bufs.at[1], self.minus)

    def direct_plus(self):
        self.dir_b = self.c.make(self.src(1, 1), self.bufs.at[3], self.plus)

    def direct_minus(self):
        self.dir_a = self.c.make(self.src(3, 0), self.bufs.at[2], self.minus)

    def acc_plus(self):
        self.two_a.wait_recv()
        ref = self.src(1, 0)
        ref[...] = ref[...] + self.bufs[0]
        self.acc_a = self.c.make(ref, self.bufs.at[4], self.plus)

    def acc_minus(self):
        self.two_b.wait_recv()
        ref = self.src(3, 1)
        ref[...] = ref[...] + self.bufs[1]
        self.acc_b = self.c.make(ref, self.bufs.at[5], self.minus)

    def final(self, half):
        direct, acc = (self.dir_a, self.acc_a) if half == 0 else (self.dir_b, self.acc_b)
        direct.wait_recv()
        acc.wait_recv()
        return self.src(0, half)[...] + self.bufs[2 + half] + self.bufs[4 + half]


def kernel(
    pre_h, up_h, gain_h, mean_h, inv_h, feat_h, og_h,
    ig_o, st_o, wg_o,
    pre, up, gain, mean, inv, feat, ft, og, ig,
    wp, wo, wd, x1, y1, x2, y2, zs, zr, wg,
    bnp, bnd, bnx, bny, bnz, bna, bnf,
    local_sem, send_sem, recv_sem, zsend, zrecv, bzsend, bzrecv, agsend, agrecv, zk,
):
    rep, zero = lax.axis_index("rep"), lax.axis_index("zero")
    y, zl = rep // NZL, lax.rem(rep, NZL)
    core = lax.rem(zero, 2)
    xq = zero // 2
    x, zh = lax.rem(xq, NX), xq // NX
    z = zh * NZL + zl

    def at(dx=0, dy=0, dz=0, dc=0):
        zz = lax.rem(z + dz + NZ, NZ)
        xx, yy = lax.rem(x + dx + NX, NX), lax.rem(y + dy + NY, NY)
        cc = lax.rem(core + dc, 2)
        return (yy * NZL + lax.rem(zz, NZL), (zz // NZL * NX + xx) * 2 + cc)

    loads = {}
    n_local = 0

    def load(name, src, dst):
        nonlocal n_local
        loads[name] = pltpu.make_async_copy(src, dst, local_sem.at[n_local])
        loads[name].start()
        n_local += 1

    load("up", up_h, up)
    load("pre", pre_h, pre)
    load("mean", mean_h, mean)
    load("inv", inv_h, inv)
    load("feat", feat_h, feat)
    offsets = (2, 1, 3, 0)
    for s in range(8):
        colour, k = s % 2, s // 2
        column = mul(colour * 1024 + lax.rem(y + offsets[k], NY) * W, W)
        load(("og", s), og_h.at[:, pl.ds(column, W)], og.at[s])
    load("gain", gain_h, gain)

    barrier = pltpu.get_barrier_semaphore()
    near = [at(dc=1), at(dz=1), at(dz=-1)]
    near += [at(dx=d) for d in (1, 2, 3)] + [at(dy=d) for d in (1, 2, 3)]
    for device in near:
        pl.semaphore_signal(barrier, inc=1, device_id=device, device_id_type=MESH)

    copies = Copies(send_sem, recv_sem)

    for name in ("up", "pre", "mean", "inv"):
        loads[name].wait()

    def sums(i, carry):
        cols = pl.ds(mul(i * 512, 512), 512)
        g = up[:, cols].astype(jnp.float32)
        n = (pre[:, cols].astype(jnp.float32) - mean[:, cols]) * inv[:, cols]
        bnp[0:1, cols] = jnp.sum(g, axis=0, keepdims=True)
        bnp[1:2, cols] = jnp.sum(g * n, axis=0, keepdims=True)
        return carry

    lax.fori_loop(0, F // 512, sums, 0)

    pl.semaphore_wait(barrier, len(near))

    def z_round(i, hop):
        for d in (hop, -hop):
            pl.semaphore_signal(zk.at[i], inc=1, device_id=at(dz=d), device_id_type=MESH)

    z_round(0, 1)

    mine = core * F_CORE
    other = (1 - core) * F_CORE
    bn_pair = copies.make(bnp.at[:, pl.ds(mul(other, F_CORE), F_CORE)], bnd, at(dc=1))

    loads["feat"].wait()
    t = feat[...].T
    for c in range(2):
        for xx in range(NX):
            for zz in range(NZH):
                dst = ((c * NX + xx) * NZH + zz) * 16
                src = ((zz * NX + xx) * 2 + c) * 16
                ft[dst : dst + 16, :] = t[src : src + 16, :]

    def product(s, c):
        left = ft[pl.ds(mul(c * 256, 256), 256), :]
        return lax.dot_general(
            left, og[s], (((1,), (0,)), ((), ())), preferred_element_type=jnp.float32
        )

    pair = []
    for s in range(8):
        loads[("og", s)].wait()
        wp[s] = product(s, 1 - core)
        pair.append(copies.make(wp.at[s], wd.at[s], at(dc=1)))

    bn_pair.wait_recv()
    half = pl.ds(mul(mine, F_CORE), F_CORE)
    bnp[:, half] = bnp[:, half] + bnd[...]

    def f_x(d):
        return pl.ds(mul(mine + lax.rem(x + d, NX) * F_X, F_X), F_X)

    bn_x = [copies.make(bnp.at[:, f_x(d)], bnx.at[d], at(dx=d)) for d in (2, 1, 3)]

    def wait_z_round(i):
        pl.semaphore_wait(zk.at[i], 2)

    wait_z_round(0)
    z_round(1, 2)

    def x_rows(xx, h, base=0):
        return pl.ds(mul(lax.rem(x + xx, NX) * 64 + h * 32, 32), 32)

    ring_x1 = [
        Ring4(
            copies,
            lambda off, h, k=k: wo.at[2 * k, x_rows(off, h)],
            x1.at[k],
            at(dx=1),
            at(dx=-1),
        )
        for k in range(4)
    ]
    order = {2: 0, 1: 1, 3: 2, 0: 3}
    ring_y1 = [
        Ring4(
            copies,
            lambda off, h, p=p: wo.at[2 * order[off] + 1, p * 128 + h * 64 : p * 128 + h * 64 + 64],
            y1.at[p],
            at(dy=1),
            at(dy=-1),
        )
        for p in range(2)
    ]
    for s in range(8):
        colour, k = s % 2, s // 2
        own = product(s, core)
        pair[s].wait_recv()
        wo[s] = own + wd[s]
        if colour == 0:
            ring_x1[k].send2()
        else:
            for ring in ring_y1:
                if k == 0:
                    ring.send2()
                elif k == 1:
                    ring.direct_plus()
                elif k == 2:
                    ring.direct_minus()

    for c in bn_x:
        c.wait_recv()
    mine_x = f_x(0)
    bnp[:, mine_x] = bnp[:, mine_x] + bnx[1] + bnx[2] + bnx[3]

    def f_y(d):
        return pl.ds(mul(mine + x * F_X + lax.rem(y + d, NY) * F_Y, F_Y), F_Y)

    bn_y = [copies.make(bnp.at[:, f_y(d)], bny.at[d], at(dy=d)) for d in (2, 1, 3)]
    wait_z_round(1)
    z_round(2, 4)

    def acc_x(k):
        ring_x1[k].acc_plus()
        ring_x1[k].acc_minus()
        ring_x1[k].direct_plus()
        ring_x1[k].direct_minus()

    def acc_y(p):
        ring_y1[p].acc_plus()
        ring_y1[p].acc_minus()

    acc_x(0)
    acc_x(1)
    acc_y(0)
    acc_x(2)
    acc_x(3)
    acc_y(1)

    for c in bn_y:
        c.wait_recv()
    wait_z_round(2)
    bnz[z] = bnp[:, f_y(0)] + bny[1] + bny[2] + bny[3]
    far = [8, 7, 9, 6, 10, 5, 11, 4, 12, 3, 13, 2, 14, 1, 15]

    def bz_copy(i, d):
        return pltpu.make_async_remote_copy(
            src_ref=bnz.at[z],
            dst_ref=bnz.at[z],
            send_sem=bzsend.at[i],
            recv_sem=bzrecv.at[i],
            device_id=at(dz=d),
            device_id_type=MESH,
        )

    def bz_arrival(i, d):
        slot = lax.rem(z - d + NZ, NZ)
        return pltpu.make_async_remote_copy(
            src_ref=bnz.at[slot],
            dst_ref=bnz.at[slot],
            send_sem=bzsend.at[i],
            recv_sem=bzrecv.at[i],
            device_id=at(dz=d),
            device_id_type=MESH,
        )

    for i, d in enumerate(far):
        bz_copy(i, d).start()

    ring_x2 = Ring4(
        copies,
        lambda off, h: wo.at[2 * order[off], x_rows(0, h)],
        x2,
        at(dy=1),
        at(dy=-1),
    )
    ring_y2 = Ring4(copies, lambda off, h: wo.at[7, x_rows(off, h)], y2, at(dx=1), at(dx=-1))

    def final_x(k):
        for h in range(2):
            wo[2 * k, x_rows(0, h)] = ring_x1[k].final(h)

    def final_y(p):
        for h in range(2):
            rows = p * 128 + h * 64
            wo[7, rows : rows + 64] = ring_y1[p].final(h)

    final_x(0)
    ring_x2.send2()
    final_x(1)
    ring_x2.direct_plus()
    final_x(2)
    ring_x2.direct_minus()
    final_y(0)
    final_y(1)
    ring_y2.send2()
    ring_y2.direct_plus()
    ring_y2.direct_minus()
    final_x(3)
    ring_x2.acc_plus()
    ring_x2.acc_minus()

    for i, d in enumerate(far):
        bz_arrival(i, d).wait_recv()
    total = bnz[0]
    for i in range(1, NZ):
        total = total + bnz[i]
    bna[:, f_y(0)] = total * (1.0 / IMAGES)
    bn_ay = [copies.make(bna.at[:, f_y(0)], bna.at[:, f_y(0)], at(dy=d)) for d in (2, 1, 3)]

    ring_y2.acc_plus()
    ring_y2.acc_minus()

    def wgt_z(colour):
        ring = ring_x2 if colour == 0 else ring_y2
        for h in range(2):
            v = ring.final(h)
            for i in range(2):
                zs[2 * colour + i, h * 32 : h * 32 + 32, :] = v[:, i * 128 : i * 128 + 128]

    def z_piece(d):
        zz = lax.rem(z + d, NZ)
        return zs.at[lax.rem(zz, NZL), pl.ds(mul(zz // NZL * 16, 16), 16)]

    def z_copy(i, d):
        return pltpu.make_async_remote_copy(
            src_ref=z_piece(d),
            dst_ref=zr.at[d],
            send_sem=zsend.at[i],
            recv_sem=zrecv.at[i],
            device_id=at(dz=d),
            device_id_type=MESH,
        )

    wgt_z(0)
    wgt_z(1)
    z_copies = [z_copy(i, d) for i, d in enumerate(far)]
    for c in z_copies:
        c.start()

    for i, d in enumerate((2, 1, 3)):
        bn_ay[i].wait_recv()
    bn_ax = [copies.make(bna.at[:, f_x(0)], bna.at[:, f_x(0)], at(dx=d)) for d in (2, 1, 3)]
    for c in bn_ax:
        c.wait_recv()
    bn_ap = copies.make(bna.at[:, half], bna.at[:, half], at(dc=1))
    bn_ap.wait_recv()
    loads["gain"].wait()

    def grads(i, carry):
        cols = pl.ds(mul(i * 512, 512), 512)
        g = up[:, cols].astype(jnp.float32)
        n = (pre[:, cols].astype(jnp.float32) - mean[:, cols]) * inv[:, cols]
        scale = gain[:, cols] * inv[:, cols]
        ig[:, cols] = (scale * (g - bna[0:1, cols] - n * bna[1:2, cols])).astype(jnp.bfloat16)
        return carry

    lax.fori_loop(0, F // 512, grads, 0)
    ig_store = pltpu.make_async_copy(ig, ig_o, local_sem.at[n_local])
    ig_store.start()
    st_store = pltpu.make_async_copy(bna, st_o, local_sem.at[n_local + 1])
    st_store.start()

    result = zs[zl, pl.ds(mul(zh * 16, 16), 16)]
    for i, d in enumerate(far):
        z_copies[i].wait_recv()
        result = result + zr[d]
    column = mul(zl // 2 * 1024 + y * W + lax.rem(zl, 2) * 128, 128)
    wg[:, pl.ds(column, 128)] = result * (1.0 / IMAGES)

    peers = [(2, 3), (2, 1), (2, 2), (1, 3), (3, 3), (1, 1), (3, 1), (1, 2), (3, 2), (2, 0), (0, 3), (0, 1), (0, 2), (1, 0), (3, 0)]

    def ag_copy(i, dy, dl, sent):
        yy, ll = (lax.rem(y + dy, NY), lax.rem(zl + dl, NZL))
        sy, sl = (y, zl) if sent else (lax.rem(y - dy + NY, NY), lax.rem(zl - dl + NZL, NZL))
        ref = wg.at[:, pl.ds(mul(sl // 2 * 1024 + sy * W + lax.rem(sl, 2) * 128, 128), 128)]
        return pltpu.make_async_remote_copy(
            src_ref=ref,
            dst_ref=ref,
            send_sem=agsend.at[i],
            recv_sem=agrecv.at[i],
            device_id=(yy * NZL + ll, zero),
            device_id_type=MESH,
        )

    for i, (dy, dl) in enumerate(peers):
        ag_copy(i, dy, dl, True).start()
    for i, (dy, dl) in enumerate(peers):
        ag_copy(i, dy, dl, False).wait_recv()
    wg_store = pltpu.make_async_copy(wg, wg_o, local_sem.at[n_local + 2])
    wg_store.start()

    for c in copies.all:
        c.wait_send()
    for i, d in enumerate(far):
        z_copies[i].wait_send()
        bz_copy(i, d).wait_send()
    for i, (dy, dl) in enumerate(peers):
        ag_copy(i, dy, dl, True).wait_send()
    ig_store.wait()
    st_store.wait()
    wg_store.wait()


N_COPIES = 96


def per_device(pre_norm, upstream, norm_gain, saved_mean, inv_std, features, out_grads):
    row = lambda v: v.reshape(1, F)
    f32, bf16 = jnp.float32, jnp.bfloat16
    vm = pltpu.VMEM
    dma = pltpu.SemaphoreType.DMA
    ig, st, wg = pl.pallas_call(
        kernel,
        out_shape=(
            jax.ShapeDtypeStruct((16, F), bf16),
            jax.ShapeDtypeStruct((2, F), f32),
            jax.ShapeDtypeStruct((16, COUT), f32),
        ),
        in_specs=[pl.BlockSpec(memory_space=pl.ANY)] * 7,
        out_specs=(pl.BlockSpec(memory_space=pl.ANY),) * 3,
        scratch_shapes=[
            vm((16, F), bf16), vm((16, F), bf16), vm((1, F), f32), vm((1, F), f32), vm((1, F), f32),
            vm((ROWS, CIN), bf16), vm((CIN, ROWS), bf16), vm((8, ROWS, W), bf16), vm((16, F), bf16),
            vm((8, 256, W), f32), vm((8, 256, W), f32), vm((8, 256, W), f32),
            vm((4, 6, 32, W), f32), vm((2, 6, 64, W), f32), vm((6, 32, W), f32), vm((6, 32, W), f32),
            vm((NZL, 64, 128), f32), vm((NZ, 16, 128), f32), vm((16, COUT), f32),
            vm((2, F), f32), vm((2, F_CORE), f32), vm((4, 2, F_X), f32), vm((4, 2, F_Y), f32),
            vm((NZ, 2, F_Y), f32), vm((2, F), f32), vm((8, 128), f32),
            dma((17,)), dma((N_COPIES,)), dma((N_COPIES,)),
            dma((15,)), dma((15,)), dma((15,)), dma((15,)), dma((15,)), dma((15,)),
            pltpu.SemaphoreType.REGULAR((3,)),
        ],
        compiler_params=pltpu.CompilerParams(
            collective_id=0, has_side_effects=True, vmem_limit_bytes=48 * 1024 * 1024
        ),
        name="twins",
    )(pre_norm, upstream, row(norm_gain), row(saved_mean), row(inv_std), features, out_grads)
    return ig, st[1], st[0], wg


def solution(mesh):
    split = P(("rep", "zero"), None)
    return jax.shard_map(
        per_device,
        mesh=mesh,
        in_specs=(split, split, P(), P(), P(), split, split),
        out_specs=(split, P(), P(), P("zero", None)),
        check_vma=False,
    )
```

time: 258 us -> 62.4 us (0.24)
  the two profiles are of different devices: /device:TPU:4 before, /device:TPU:8 now
where the time goes in v1:
time: 62.4 us; the launch traced here: 61.9 us
  Pallas kernels  52 us (83%)
  local copies, waits for them, and re-layouts  9.24 us (15%)
  between operations  0.66 us (1%)
    pallas_call x1, Pallas kernels, per_device(): pl.pallas_call(kernel, out_shape=(jax.ShapeDtypeStruct((16, F), bf16), ja...  52 us
    unnamed x16, local copies, waits for them, and re-layouts  8.57 us

profile of v1, /device:TPU:8, one launch (start us, length us, event | category | flops | bytes accessed | tf_op | source)
XLA Modules:
  0.0 61.9 jit_solution(15001410434598447134)
XLA Ops:
  0.6 0.0 copy-start
  0.6 1.9 %copy-done = bf16[784,2048]{1,0:T(8,128)(2,1)S(1)} copy-done((bf16[784,2048]{1,0:T(8,128)(2,1)S(1)}, bf16[784,2048]{1,0:T(8,128)(2,1)}, u32[]{:S(2)}) %copy-start) | copy-done | bytes 3211288
  2.5 0.0 copy-start.1
  2.5 1.1 %copy-done.1 = bf16[784,512]{1,0:T(8,128)(2,1)S(1)} copy-done((bf16[784,512]{1,0:T(8,128)(2,1)S(1)}, bf16[784,512]{1,0:T(8,128)(2,1)}, u32[]{:S(2)}) %copy-start.1) | copy-done | bytes 802840
  3.7 0.0 copy-start.2
  3.7 0.9 %copy-done.2 = bf16[16,8192]{1,0:T(8,128)(2,1)S(1)} copy-done((bf16[16,8192]{1,0:T(8,128)(2,1)S(1)}, bf16[16,8192]{1,0:T(8,128)(2,1)}, u32[]{:S(2)}) %copy-start.2) | copy-done | bytes 262168
  4.6 0.0 copy-start.3
  4.6 0.9 %copy-done.3 = bf16[16,8192]{1,0:T(8,128)(2,1)S(1)} copy-done((bf16[16,8192]{1,0:T(8,128)(2,1)S(1)}, bf16[16,8192]{1,0:T(8,128)(2,1)}, u32[]{:S(2)}) %copy-start.3) | copy-done | bytes 262168
  5.6 0.0 copy-start.4
  5.6 0.8 %copy-done.4 = f32[8192]{0:T(1024)S(1)} copy-done((f32[8192]{0:T(1024)S(1)}, f32[8192]{0:T(1024)}, u32[]{:S(2)}) %copy-start.4) | copy-done | bytes 32792
  6.3 0.0 copy-start.5
  6.3 0.8 %copy-done.5 = f32[8192]{0:T(1024)S(1)} copy-done((f32[8192]{0:T(1024)S(1)}, f32[8192]{0:T(1024)}, u32[]{:S(2)}) %copy-start.5) | copy-done | bytes 32792
  7.1 0.0 copy-start.6
  7.1 0.8 %copy-done.6 = f32[8192]{0:T(1024)S(1)} copy-done((f32[8192]{0:T(1024)S(1)}, f32[8192]{0:T(1024)}, u32[]{:S(2)}) %copy-start.6) | copy-done | bytes 32792
  7.9 52.0 %twins.1 = (bf16[16,8192]{1,0:T(8,128)(2,1)S(1)}, f32[2,8192]{1,0:T(2,128)S(1)}, f32[16,2048]{1,0:T(8,128)S(1)}) custom-call(bf16[16,8192]{1,0:T(8,128)(2,1)S(1)} %copy-done.2, bf16[16,8192]{1,0:T(8,128)(2,1)S(1)} %copy-done.3, f32[1,8192]{1,0:T(1,128)S(1)} %bitcast.5, f32[1,8192]{1,0:T(1,128)S(1)} %bitcast.6, f32[1,8192]{1,0:T(1,128)S(1)} %bitcast.7, ...), custom_call_target="tpu_custom_call" | custom-call | tf_op jit(solution)/shard_map/twins/pallas_call | solution.py:432
  59.9 0.7 %fusion = (f32[1,8192]{1,0:T(1,128)}, f32[1,8192]{1,0:T(1,128)}) fusion(f32[2,8192]{1,0:T(2,128)S(1)} %get-tuple-element.8), kind=kLoop, calls=%fused_computation | loop fusion | bytes 131072 | tf_op jit(solution)/shard_map/slice | solution.py:458
  60.6 0.7 %copy.13 = bf16[16,8192]{1,0:T(8,128)(2,1)} copy(bf16[16,8192]{1,0:T(8,128)(2,1)S(1)} %get-tuple-element.16) | data formatting | bytes 524288
  61.3 0.7 %copy.14 = f32[16,2048]{1,0:T(8,128)} copy(f32[16,2048]{1,0:T(8,128)S(1)} %get-tuple-element.19) | data formatting | bytes 262144
Async XLA Ops:
  0.6 1.9 %copy-start = (bf16[784,2048]{1,0:T(8,128)(2,1)S(1)}, bf16[784,2048]{1,0:T(8,128)(2,1)}, u32[]{:S(2)}) copy-start(bf16[784,2048]{1,0:T(8,128)(2,1)} %og_h.1) | copy-start | bytes 9633796
  2.5 1.1 %copy-start.1 = (bf16[784,512]{1,0:T(8,128)(2,1)S(1)}, bf16[784,512]{1,0:T(8,128)(2,1)}, u32[]{:S(2)}) copy-start(bf16[784,512]{1,0:T(8,128)(2,1)} %feat_h.1) | copy-start | bytes 2408452
  3.7 0.9 %copy-start.2 = (bf16[16,8192]{1,0:T(8,128)(2,1)S(1)}, bf16[16,8192]{1,0:T(8,128)(2,1)}, u32[]{:S(2)}) copy-start(bf16[16,8192]{1,0:T(8,128)(2,1)} %pre_h.1) | copy-start | bytes 786436
  4.6 0.9 %copy-start.3 = (bf16[16,8192]{1,0:T(8,128)(2,1)S(1)}, bf16[16,8192]{1,0:T(8,128)(2,1)}, u32[]{:S(2)}) copy-start(bf16[16,8192]{1,0:T(8,128)(2,1)} %up_h.1) | copy-start | bytes 786436
  5.6 0.8 %copy-start.4 = (f32[8192]{0:T(1024)S(1)}, f32[8192]{0:T(1024)}, u32[]{:S(2)}) copy-start(f32[8192]{0:T(1024)} %param.9) | copy-start | bytes 98308
  6.3 0.8 %copy-start.5 = (f32[8192]{0:T(1024)S(1)}, f32[8192]{0:T(1024)}, u32[]{:S(2)}) copy-start(f32[8192]{0:T(1024)} %param.10) | copy-start | bytes 98308
  7.1 0.8 %copy-start.6 = (f32[8192]{0:T(1024)S(1)}, f32[8192]{0:T(1024)}, u32[]{:S(2)}) copy-start(f32[8192]{0:T(1024)} %param.11) | copy-start | bytes 98308

commit v2 on v1

v2 whole, which is shorter than its diff:
```python
import functools

import jax
import jax.numpy as jnp
from jax import lax
from jax.experimental import pallas as pl
from jax.experimental.pallas import tpu as pltpu
from jax.sharding import PartitionSpec as P

MESH = pl.DeviceIdType.MESH
F = 8192
ROWS = 784
CIN = 512
COUT = 2048
IMAGES = 8192
NX, NY, NZL, NZH = 4, 4, 4, 4
NZ = NZL * NZH
W = 256
F_CORE, F_X, F_Y = F // 2, F // 8, F // 32


def mul(v, m):
    return pl.multiple_of(v, m)


class Phases:
    def __init__(self):
        self.open = None

    def __call__(self, name):
        if self.open is not None:
            self.open.__exit__(None, None, None)
        self.open = None
        if name is not None:
            self.open = jax.named_scope(name)
            self.open.__enter__()


class Copies:
    def __init__(self, send, recv):
        self.send, self.recv, self.n, self.all = send, recv, 0, []

    def make(self, src, dst, device):
        i = self.n
        self.n += 1
        copy = pltpu.make_async_remote_copy(
            src_ref=src,
            dst_ref=dst,
            send_sem=self.send.at[i],
            recv_sem=self.recv.at[i],
            device_id=device,
            device_id_type=MESH,
        )
        copy.start()
        self.all.append(copy)
        return copy


class Ring4:
    def __init__(self, copies, src, bufs, plus, minus):
        self.c, self.src, self.bufs, self.plus, self.minus = copies, src, bufs, plus, minus

    def send2(self):
        self.two_a = self.c.make(self.src(2, 0), self.bufs.at[0], self.plus)
        self.two_b = self.c.make(self.src(2, 1), self.bufs.at[1], self.minus)

    def direct_plus(self):
        self.dir_b = self.c.make(self.src(1, 1), self.bufs.at[3], self.plus)

    def direct_minus(self):
        self.dir_a = self.c.make(self.src(3, 0), self.bufs.at[2], self.minus)

    def acc_plus(self):
        self.two_a.wait_recv()
        ref = self.src(1, 0)
        ref[...] = ref[...] + self.bufs[0]
        self.acc_a = self.c.make(ref, self.bufs.at[4], self.plus)

    def acc_minus(self):
        self.two_b.wait_recv()
        ref = self.src(3, 1)
        ref[...] = ref[...] + self.bufs[1]
        self.acc_b = self.c.make(ref, self.bufs.at[5], self.minus)

    def final(self, half):
        direct, acc = (self.dir_a, self.acc_a) if half == 0 else (self.dir_b, self.acc_b)
        direct.wait_recv()
        acc.wait_recv()
        return self.src(0, half)[...] + self.bufs[2 + half] + self.bufs[4 + half]


def kernel(
    pre_h, up_h, gain_h, mean_h, inv_h, feat_h, og_h,
    ig, gain_o, bias_o, wg,
    pre, up, gain, mean, inv, feat, ft, og,
    wp, wo, wd, x1, y1, x2, y2, zs, zr,
    bnp, bnd, bnx, bnz, bna,
    local_sem, send_sem, recv_sem, zsend, zrecv, bzsend, bzrecv, agsend, agrecv, zk,
):
    rep, zero = lax.axis_index("rep"), lax.axis_index("zero")
    y, zl = rep // NZL, lax.rem(rep, NZL)
    core = lax.rem(zero, 2)
    xq = zero // 2
    x, zh = lax.rem(xq, NX), xq // NX
    z = zh * NZL + zl

    def at(dx=0, dy=0, dz=0, dc=0):
        zz = lax.rem(z + dz + NZ, NZ)
        xx, yy = lax.rem(x + dx + NX, NX), lax.rem(y + dy + NY, NY)
        cc = lax.rem(core + dc, 2)
        return (yy * NZL + lax.rem(zz, NZL), (zz // NZL * NX + xx) * 2 + cc)

    phase = Phases()
    phase("start")
    loads = {}
    n_local = 0

    def load(name, src, dst):
        nonlocal n_local
        loads[name] = pltpu.make_async_copy(src, dst, local_sem.at[n_local])
        loads[name].start()
        n_local += 1

    load("feat", feat_h, feat)
    load("up", up_h, up)
    load("pre", pre_h, pre)
    load("mean", mean_h, mean)
    load("inv", inv_h, inv)
    offsets = (2, 1, 3, 0)
    for s in range(8):
        colour, k = s % 2, s // 2
        column = mul(colour * 1024 + lax.rem(y + offsets[k], NY) * W, W)
        load(
            ("og", s),
            og_h.at[:, pl.ds(column, W)],
            og.at[s // 4, :, s % 4 * W : s % 4 * W + W],
        )
    load("gain", gain_h, gain)

    barrier = pltpu.get_barrier_semaphore()
    plane = [(2, 2), (2, 1), (2, 3), (1, 2), (3, 2), (1, 1), (1, 3), (3, 1), (3, 3)]
    plane += [(2, 0), (0, 2), (1, 0), (3, 0), (0, 1), (0, 3)]
    near = [at(dc=1), at(dz=1), at(dz=-1)] + [at(dx=dx, dy=dy) for dx, dy in plane]
    for device in near:
        pl.semaphore_signal(barrier, inc=1, device_id=device, device_id_type=MESH)

    copies = Copies(send_sem, recv_sem)

    phase("featwait")
    loads["feat"].wait()
    phase("transpose")
    t = feat[...].T
    for c in range(2):
        for xx in range(NX):
            for zz in range(NZH):
                dst = ((c * NX + xx) * NZH + zz) * 16
                src = ((zz * NX + xx) * 2 + c) * 16
                ft[dst : dst + 16, :] = t[src : src + 16, :]

    phase("bnload")
    for name in ("up", "pre", "mean", "inv"):
        loads[name].wait()

    phase("bnsum")
    def sums(i, carry):
        cols = pl.ds(mul(i * 512, 512), 512)
        g = up[:, cols].astype(jnp.float32)
        n = (pre[:, cols].astype(jnp.float32) - mean[:, cols]) * inv[:, cols]
        bnp[0:1, cols] = jnp.sum(g, axis=0, keepdims=True)
        bnp[1:2, cols] = jnp.sum(g * n, axis=0, keepdims=True)
        return carry

    lax.fori_loop(0, F // 512, sums, 0)

    phase("barrier")
    pl.semaphore_wait(barrier, len(near))

    def z_round(i, hop):
        for d in (hop, -hop):
            pl.semaphore_signal(zk.at[i], inc=1, device_id=at(dz=d), device_id_type=MESH)

    z_round(0, 1)

    mine = core * F_CORE
    other = (1 - core) * F_CORE
    bn_pair = copies.make(bnp.at[:, pl.ds(mul(other, F_CORE), F_CORE)], bnd, at(dc=1))

    phase("products")
    def product(part, c, out):
        left = ft[pl.ds(mul(c * 256, 256), 256), :]
        v = lax.dot_general(
            left, og[part], (((1,), (0,)), ((), ())), preferred_element_type=jnp.float32
        )
        for i in range(4):
            out[4 * part + i] = v[:, i * W : i * W + W]

    pair = []
    for part in range(2):
        for i in range(4):
            loads[("og", 4 * part + i)].wait()
        product(part, 1 - core, wp)
        for i in range(4):
            s = 4 * part + i
            pair.append(copies.make(wp.at[s], wd.at[s], at(dc=1)))

    phase("bnpair")
    bn_pair.wait_recv()
    half = pl.ds(mul(mine, F_CORE), F_CORE)
    bnp[:, half] = bnp[:, half] + bnd[...]

    def f_xy(dx, dy):
        start = mine + lax.rem(x + dx, NX) * F_X + lax.rem(y + dy, NY) * F_Y
        return pl.ds(mul(start, F_Y), F_Y)

    bn_xy = [
        copies.make(bnp.at[:, f_xy(dx, dy)], bnx.at[4 * dx + dy], at(dx=dx, dy=dy))
        for dx, dy in plane
    ]

    def wait_z_round(i):
        pl.semaphore_wait(zk.at[i], 2)

    wait_z_round(0)
    z_round(1, 2)

    phase("own")
    def x_rows(xx, h, base=0):
        return pl.ds(mul(lax.rem(x + xx, NX) * 64 + h * 32, 32), 32)

    ring_x1 = [
        Ring4(
            copies,
            lambda off, h, k=k: wo.at[2 * k, x_rows(off, h)],
            x1.at[k],
            at(dx=1),
            at(dx=-1),
        )
        for k in range(4)
    ]
    order = {2: 0, 1: 1, 3: 2, 0: 3}
    ring_y1 = [
        Ring4(
            copies,
            lambda off, h, p=p: wo.at[2 * order[off] + 1, p * 128 + h * 64 : p * 128 + h * 64 + 64],
            y1.at[p],
            at(dy=1),
            at(dy=-1),
        )
        for p in range(2)
    ]
    for s in range(8):
        colour, k = s % 2, s // 2
        if s % 4 == 0:
            phase(f"own{s // 4}")
            product(s // 4, core, wo)
        phase(f"pairwait{s}")
        pair[s].wait_recv()
        phase(f"add{s}")
        wo[s] = wo[s] + wd[s]
        if colour == 0:
            ring_x1[k].send2()
        else:
            for ring in ring_y1:
                if k == 0:
                    ring.send2()
                elif k == 1:
                    ring.direct_plus()
                elif k == 2:
                    ring.direct_minus()
    wait_z_round(1)
    z_round(2, 4)

    def acc_x(k):
        ring_x1[k].acc_plus()
        ring_x1[k].acc_minus()
        ring_x1[k].direct_plus()
        ring_x1[k].direct_minus()

    def acc_y(p):
        ring_y1[p].acc_plus()
        ring_y1[p].acc_minus()

    phase("accx0")
    acc_x(0)
    phase("accx1")
    acc_x(1)
    phase("bnxy")
    for c in bn_xy:
        c.wait_recv()
    wait_z_round(2)
    total = bnp[:, f_xy(0, 0)]
    for dx, dy in plane:
        total = total + bnx[4 * dx + dy]
    bnz[z] = total
    far = [8, 7, 9, 6, 10, 5, 11, 4, 12, 3, 13, 2, 14, 1, 15]

    def bz_copy(i, d):
        return pltpu.make_async_remote_copy(
            src_ref=bnz.at[z],
            dst_ref=bnz.at[z],
            send_sem=bzsend.at[i],
            recv_sem=bzrecv.at[i],
            device_id=at(dz=d),
            device_id_type=MESH,
        )

    def bz_arrival(i, d):
        slot = lax.rem(z - d + NZ, NZ)
        return pltpu.make_async_remote_copy(
            src_ref=bnz.at[slot],
            dst_ref=bnz.at[slot],
            send_sem=bzsend.at[i],
            recv_sem=bzrecv.at[i],
            device_id=at(dz=d),
            device_id_type=MESH,
        )

    for i, d in enumerate(far):
        bz_copy(i, d).start()

    phase("accy0")
    acc_y(0)
    phase("accx2")
    acc_x(2)
    phase("accx3")
    acc_x(3)
    phase("accy1")
    acc_y(1)

    ring_x2 = Ring4(
        copies,
        lambda off, h: wo.at[2 * order[off], x_rows(0, h)],
        x2,
        at(dy=1),
        at(dy=-1),
    )
    ring_y2 = Ring4(copies, lambda off, h: wo.at[7, x_rows(off, h)], y2, at(dx=1), at(dx=-1))

    def final_x(k):
        for h in range(2):
            wo[2 * k, x_rows(0, h)] = ring_x1[k].final(h)

    def final_y(p):
        for h in range(2):
            rows = p * 128 + h * 64
            wo[7, rows : rows + 64] = ring_y1[p].final(h)

    phase("finx0")
    final_x(0)
    ring_x2.send2()
    phase("finx1")
    final_x(1)
    ring_x2.direct_plus()
    phase("finx2")
    final_x(2)
    ring_x2.direct_minus()
    phase("finy0")
    final_y(0)
    phase("finy1")
    final_y(1)
    ring_y2.send2()
    ring_y2.direct_plus()
    ring_y2.direct_minus()
    phase("finx3")
    final_x(3)
    phase("accx2s")
    ring_x2.acc_plus()
    ring_x2.acc_minus()

    def z_copy(colour, j):
        ll = 2 * colour + j % 2
        hh = lax.rem(zh + offsets[j // 2], NZH)
        copy = pltpu.make_async_remote_copy(
            src_ref=zs.at[ll, pl.ds(mul(hh * 16, 16), 16)],
            dst_ref=zr.at[z],
            send_sem=zsend.at[8 * colour + j],
            recv_sem=zrecv.at[z],
            device_id=(y * NZL + ll, (hh * NX + x) * 2 + core),
            device_id_type=MESH,
        )
        return copy, (None if j < 6 else ll != zl)

    def each_z(colour, act):
        for j in range(8):
            copy, guard = z_copy(colour, j)
            if guard is None:
                act(copy)
            else:
                pl.when(guard)(lambda copy=copy: act(copy))

    def weight_z(colour):
        ring = ring_x2 if colour == 0 else ring_y2
        for h in range(2):
            v = ring.final(h)
            for i in range(2):
                zs[2 * colour + i, h * 32 : h * 32 + 32, :] = v[:, i * 128 : i * 128 + 128]
        each_z(colour, lambda copy: copy.start())

    phase("wgtz0")
    weight_z(0)
    phase("accy2s")
    ring_y2.acc_plus()
    ring_y2.acc_minus()
    phase("bnz")
    for i, d in enumerate(far):
        bz_arrival(i, d).wait_recv()
    total = bnz[0]
    for i in range(1, NZ):
        total = total + bnz[i]
    bna[:, f_xy(0, 0)] = total * (1.0 / IMAGES)
    bn_axy = [
        copies.make(bna.at[:, f_xy(0, 0)], bna.at[:, f_xy(0, 0)], at(dx=dx, dy=dy))
        for dx, dy in plane
    ]

    phase("wgtz1")
    weight_z(1)

    phase("bngxy")
    for i, (dx, dy) in enumerate(plane):
        bn_axy[i].wait_recv()
    bn_ap = copies.make(bna.at[:, half], bna.at[:, half], at(dc=1))

    phase("zwait")
    result = zs[zl, pl.ds(mul(zh * 16, 16), 16)]
    for d in far:
        slot = lax.rem(z - d + NZ, NZ)
        pltpu.make_async_remote_copy(
            src_ref=zr.at[slot],
            dst_ref=zr.at[slot],
            send_sem=zsend.at[0],
            recv_sem=zrecv.at[slot],
            device_id=at(dz=d),
            device_id_type=MESH,
        ).wait_recv()
        result = result + zr[slot]
    column = mul(zl // 2 * 1024 + y * W + lax.rem(zl, 2) * 128, 128)
    wg[:, pl.ds(column, 128)] = result * (1.0 / IMAGES)

    phase("ag")
    peers = [(2, 3), (2, 1), (2, 2), (1, 3), (3, 3), (1, 1), (3, 1), (1, 2), (3, 2), (2, 0), (0, 3), (0, 1), (0, 2), (1, 0), (3, 0)]

    def ag_copy(i, dy, dl, sent):
        yy, ll = (lax.rem(y + dy, NY), lax.rem(zl + dl, NZL))
        sy, sl = (y, zl) if sent else (lax.rem(y - dy + NY, NY), lax.rem(zl - dl + NZL, NZL))
        ref = wg.at[:, pl.ds(mul(sl // 2 * 1024 + sy * W + lax.rem(sl, 2) * 128, 128), 128)]
        return pltpu.make_async_remote_copy(
            src_ref=ref,
            dst_ref=ref,
            send_sem=agsend.at[i],
            recv_sem=agrecv.at[i],
            device_id=(yy * NZL + ll, zero),
            device_id_type=MESH,
        )

    for i, (dy, dl) in enumerate(peers):
        ag_copy(i, dy, dl, True).start()
    phase("bngp")
    bn_ap.wait_recv()
    loads["gain"].wait()
    phase("grads")

    def grads(i, carry):
        cols = pl.ds(mul(i * 512, 512), 512)
        g = up[:, cols].astype(jnp.float32)
        n = (pre[:, cols].astype(jnp.float32) - mean[:, cols]) * inv[:, cols]
        scale = gain[:, cols] * inv[:, cols]
        bias_grad, gain_grad = bna[0:1, cols], bna[1:2, cols]
        bias_o[:, cols] = bias_grad
        gain_o[:, cols] = gain_grad
        ig[:, cols] = (scale * (g - bias_grad - n * gain_grad)).astype(jnp.bfloat16)
        return carry

    lax.fori_loop(0, F // 512, grads, 0)
    phase("agwait")
    for i, (dy, dl) in enumerate(peers):
        ag_copy(i, dy, dl, False).wait_recv()
    phase("drain")
    for c in copies.all:
        c.wait_send()
    for colour in range(2):
        each_z(colour, lambda copy: copy.wait_send())
    for i, d in enumerate(far):
        bz_copy(i, d).wait_send()
    for i, (dy, dl) in enumerate(peers):
        ag_copy(i, dy, dl, True).wait_send()
    phase(None)


N_COPIES = 96


def store(ig, gain, bias, wg, ig_o, gain_o, bias_o, wg_o, sem):
    pairs = ((ig, ig_o), (wg, wg_o), (gain, gain_o), (bias, bias_o))
    copies = [pltpu.make_async_copy(a, b, sem.at[i]) for i, (a, b) in enumerate(pairs)]
    for copy in copies:
        copy.start()
    for copy in copies:
        copy.wait()


def per_device(pre_norm, upstream, norm_gain, saved_mean, inv_std, features, out_grads):
    row = lambda v: v.reshape(1, F)
    f32, bf16 = jnp.float32, jnp.bfloat16
    vm = pltpu.VMEM
    dma = pltpu.SemaphoreType.DMA
    outs = (
        jax.ShapeDtypeStruct((16, F), bf16),
        jax.ShapeDtypeStruct((1, F), f32),
        jax.ShapeDtypeStruct((1, F), f32),
        jax.ShapeDtypeStruct((16, COUT), f32),
    )
    vectors = (row(norm_gain), row(saved_mean), row(inv_std))
    arrays = (pre_norm, upstream, *vectors, features, out_grads)
    results = pl.pallas_call(
        kernel,
        out_shape=outs,
        in_specs=[pl.BlockSpec(memory_space=pltpu.HBM)] * 7,
        out_specs=(pl.BlockSpec(memory_space=vm),) * 4,
        scratch_shapes=[
            vm((16, F), bf16), vm((16, F), bf16), vm((1, F), f32), vm((1, F), f32), vm((1, F), f32),
            vm((ROWS, CIN), bf16), vm((CIN, ROWS), bf16), vm((2, ROWS, 4 * W), bf16),
            vm((8, 256, W), f32), vm((8, 256, W), f32), vm((8, 256, W), f32),
            vm((4, 6, 32, W), f32), vm((2, 6, 64, W), f32), vm((6, 32, W), f32), vm((6, 32, W), f32),
            vm((NZL, 64, 128), f32), vm((NZ, 16, 128), f32),
            vm((2, F), f32), vm((2, F_CORE), f32), vm((16, 2, F_Y), f32),
            vm((NZ, 2, F_Y), f32), vm((2, F), f32),
            dma((14,)), dma((N_COPIES,)), dma((N_COPIES,)),
            dma((16,)), dma((16,)), dma((15,)), dma((15,)), dma((15,)), dma((15,)),
            pltpu.SemaphoreType.REGULAR((3,)),
        ],
        compiler_params=pltpu.CompilerParams(
            collective_id=0, has_side_effects=True, vmem_limit_bytes=32 * 1024 * 1024
        ),
        name="twins",
    )(*(pltpu.with_memory_space_constraint(v, pltpu.HBM) for v in arrays))
    ig, gain_grad, bias_grad, wg = pl.pallas_call(
        store,
        out_shape=outs,
        in_specs=[pl.BlockSpec(memory_space=pl.ANY)] * 4,
        out_specs=(pl.BlockSpec(memory_space=pltpu.HBM),) * 4,
        scratch_shapes=[dma((4,))],
        name="store",
    )(*(pltpu.with_memory_space_constraint(v, vm) for v in results))
    return ig, gain_grad.reshape(F), bias_grad.reshape(F), wg


def solution(mesh):
    split = P(("rep", "zero"), None)
    return jax.shard_map(
        per_device,
        mesh=mesh,
        in_specs=(split, split, P(), P(), P(), split, split),
        out_specs=(split, P(), P(), P("zero", None)),
        check_vma=False,
    )
```

time: 62.4 us -> 51.9 us (0.83)
  the two profiles are of different devices: /device:TPU:8 before, /device:TPU:2 now
where the time goes in v2:
time: 51.9 us; the launch traced here: 51.8 us
  Pallas kernels  51.2 us (99%)
  between operations  0.64 us (1%)
    pallas_call x1, Pallas kernels, per_device(): pl.pallas_call(kernel, out_shape=outs, in_specs=[pl.BlockSpec(memory_spac...  50.4 us

profile of v2, /device:TPU:2, one launch (start us, length us, event | category | flops | bytes accessed | tf_op | source)
XLA Modules:
  0.0 51.8 jit_solution(2425743339914108092)
XLA Ops:
  0.6 50.4 %twins.1 = (bf16[16,8192]{1,0:T(8,128)(2,1)S(1)}, f32[1,8192]{1,0:T(1,128)S(1)}, f32[1,8192]{1,0:T(1,128)S(1)}, f32[16,2048]{1,0:T(8,128)S(1)}) custom-call(bf16[16,8192]{1,0:T(8,128)(2,1)} %pre_h.1, bf16[16,8192]{1,0:T(8,128)(2,1)} %up_h.1, f32[1,8192]{1,0:T(1,128)} %bitcast.5, f32[1,8192]{1,0:T(1,128)} %bitcast.6, f32[1,8192]{1,0:T(1,128)} %bitcast.7, ...), custom_call_target="tpu_custom_call" | custom-call | tf_op jit(solution)/shard_map/twins/pallas_call | solution.py:515
  51.0 0.8 %store.1 = (bf16[16,8192]{1,0:T(8,128)(2,1)}, f32[1,8192]{1,0:T(1,128)}, f32[1,8192]{1,0:T(1,128)}, f32[16,2048]{1,0:T(8,128)}) custom-call(bf16[16,8192]{1,0:T(8,128)(2,1)S(1)} %get-tuple-element.12.ig, f32[1,8192]{1,0:T(1,128)S(1)} %get-tuple-element.13.gain, f32[1,8192]{1,0:T(1,128)S(1)} %get-tuple-element.14.bias, f32[16,2048]{1,0:T(8,128)S(1)} %get-tuple-element.15.wg), custom_call_target="tpu_custom_call" | custom-call | tf_op jit(solution)/shard_map/store/pallas_call | solution.py:537

commit v3 on v0

v3 whole, which is shorter than its diff:
```python
import functools

import jax
import jax.numpy as jnp
from jax import lax
from jax.experimental import pallas as pl
from jax.experimental.pallas import tpu as pltpu
from jax.sharding import PartitionSpec as P

MESH = pl.DeviceIdType.MESH
F = 8192
ROWS = 784
CIN = 512
COUT = 2048
IMAGES = 8192
NX, NY, NZL, NZH = 4, 4, 4, 4
NZ = NZL * NZH
W = 256
F_CORE, F_X, F_Y = F // 2, F // 8, F // 32


def mul(v, m):
    return pl.multiple_of(v, m)


class Phases:
    def __init__(self):
        self.open = None

    def __call__(self, name):
        if self.open is not None:
            self.open.__exit__(None, None, None)
        self.open = None
        if name is not None:
            self.open = jax.named_scope(name)
            self.open.__enter__()


class Copies:
    def __init__(self, send, recv, partner):
        self.send, self.recv, self.partner = send, recv, partner
        self.sends, self.n_recv = [], 0

    def group(self, whole):
        self.sends.append(whole)
        return len(self.sends) - 1

    def arrivals(self, n=1):
        self.n_recv += n
        return self.n_recv - n

    def make(self, src, dst, device, group, arrival):
        return pltpu.make_async_remote_copy(
            src_ref=src,
            dst_ref=dst,
            send_sem=self.send.at[group],
            recv_sem=self.recv.at[arrival],
            device_id=device,
            device_id_type=MESH,
        )

    def start(self, *args):
        self.make(*args).start()

    def wait(self, whole, arrival):
        self.make(whole, whole, self.partner, 0, arrival).wait_recv()

    def drain(self):
        for i, whole in enumerate(self.sends):
            self.make(whole, whole, self.partner, i, 0).wait_send()


class Ring4:
    def __init__(self, copies, group, src, bufs, plus, minus):
        self.c, self.group, self.src, self.bufs = copies, group, src, bufs
        self.plus, self.minus = plus, minus
        self.arrival = copies.arrivals(3)

    def copy(self, ref, slot, device, arrival):
        self.c.start(ref, self.bufs.at[slot], device, self.group, self.arrival + arrival)

    def send2(self):
        self.copy(self.src(2, 0), 0, self.plus, 0)
        self.copy(self.src(2, 1), 1, self.minus, 1)

    def direct_plus(self):
        self.copy(self.src(1, 1), 3, self.plus, 2)

    def direct_minus(self):
        self.copy(self.src(3, 0), 2, self.minus, 2)

    def acc(self, half):
        self.c.wait(self.bufs.at[half], self.arrival + half)
        ref = self.src(1 if half == 0 else 3, half)
        ref[...] = ref[...] + self.bufs[half]
        self.copy(ref, 4 + half, self.plus if half == 0 else self.minus, 2)

    def final(self):
        self.c.wait(self.bufs.at[2:6], self.arrival + 2)
        return [self.src(0, h)[...] + self.bufs[2 + h] + self.bufs[4 + h] for h in range(2)]


def kernel(
    pre_h, up_h, gain_h, mean_h, inv_h, feat_h, og_h,
    ig, gain_o, bias_o, wg,
    pre, up, gain, mean, inv, feat, og,
    wb, wd, x1, y1, x2, y2, zs, zr,
    bnp, bnd, bnx, bnz, bna,
    local_sem, send_sem, recv_sem, know,
):
    rep, zero = lax.axis_index("rep"), lax.axis_index("zero")
    y, zl = rep // NZL, lax.rem(rep, NZL)
    core = lax.rem(zero, 2)
    xq = zero // 2
    x, zh = lax.rem(xq, NX), xq // NX
    z = zh * NZL + zl

    def at(dx=0, dy=0, dz=0, dc=0):
        zz = lax.rem(z + dz + NZ, NZ)
        xx, yy = lax.rem(x + dx + NX, NX), lax.rem(y + dy + NY, NY)
        cc = lax.rem(core + dc, 2)
        return (yy * NZL + lax.rem(zz, NZL), (zz // NZL * NX + xx) * 2 + cc)

    phase = Phases()
    phase("start")
    loads = {}

    def load(name, src, dst):
        loads[name] = pltpu.make_async_copy(src, dst, local_sem.at[len(loads)])
        loads[name].start()

    load("up", up_h, up)
    load("pre", pre_h, pre)
    load("mean", mean_h, mean)
    load("inv", inv_h, inv)
    load("feat", feat_h, feat)
    offsets = (2, 1, 3, 0)
    for k in range(4):
        for colour in range(2):
            column = mul(colour * 1024 + lax.rem(y + offsets[k], NY) * W, W)
            dst = og.at[k, :, colour * W : colour * W + W]
            load(("og", 2 * k + colour), og_h.at[:, pl.ds(column, W)], dst)
    load("gain", gain_h, gain)

    def signal(sem, device):
        pl.semaphore_signal(sem, inc=1, device_id=device, device_id_type=MESH)

    barrier = pltpu.get_barrier_semaphore()
    beside = [at(dx=1), at(dx=-1), at(dy=1), at(dy=-1)]
    near = [at(dc=1), at(dz=1), at(dz=-1)] + beside
    for device in near:
        signal(barrier, device)
    plane = [(2, 2), (2, 1), (2, 3), (1, 2), (3, 2), (1, 1), (1, 3), (3, 1), (3, 3)]
    plane += [(2, 0), (0, 2), (1, 0), (3, 0), (0, 1), (0, 3)]
    far = [8, 7, 9, 6, 10, 5, 11, 4, 12, 3, 13, 2, 14, 1, 15]

    copies = Copies(send_sem, recv_sem, at(dc=1))
    mine = core * F_CORE
    other = (1 - core) * F_CORE
    half = pl.ds(mul(mine, F_CORE), F_CORE)

    phase("bnload")
    for name in ("up", "pre", "mean", "inv"):
        loads[name].wait()

    def sums(i, carry):
        cols = pl.ds(mul(i * 512, 512), 512)
        g = up[:, cols].astype(jnp.float32)
        n = (pre[:, cols].astype(jnp.float32) - mean[:, cols]) * inv[:, cols]
        bnp[0:1, cols] = jnp.sum(g, axis=0, keepdims=True)
        bnp[1:2, cols] = jnp.sum(g * n, axis=0, keepdims=True)
        return carry

    phase("bnsum")
    lax.fori_loop(0, F // 512, sums, 0)
    phase("featwait")
    loads["feat"].wait()

    def product(k):
        loads[("og", 2 * k)].wait()
        loads[("og", 2 * k + 1)].wait()
        v = lax.dot_general(
            feat[...], og[k], (((0,), (0,)), ((), ())), preferred_element_type=jnp.float32
        )
        for c in range(2):
            for xx in range(NX):
                for zz in range(NZH):
                    dst = (xx * NZH + zz) * 16
                    src = ((zz * NX + xx) * 2 + c) * 16
                    for i in range(2):
                        wb[c, 2 * k + i, dst : dst + 16, :] = v[
                            src : src + 16, i * W : i * W + W
                        ]

    pair_group = copies.group(wd)
    pair = copies.arrivals(8)

    def pair_send(k):
        for s in (2 * k, 2 * k + 1):
            copies.start(wb.at[1 - core, s], wd.at[s], at(dc=1), pair_group, pair + s)

    phase("prod0")
    product(0)
    phase("barrier")
    pl.semaphore_wait(barrier, len(near))
    for device in beside:
        signal(know.at[3], device)
    for d in (1, -1):
        signal(know.at[0], at(dz=d))
    pair_send(0)
    bn_pair = copies.arrivals()
    copies.start(
        bnp.at[:, pl.ds(mul(other, F_CORE), F_CORE)], bnd, at(dc=1), copies.group(bnd), bn_pair
    )
    phase("prod1")
    product(1)
    pair_send(1)
    phase("prod2")
    product(2)
    pair_send(2)

    def x_rows(xx, h):
        return pl.ds(mul(lax.rem(x + xx, NX) * 64 + h * 32, 32), 32)

    order = {2: 0, 1: 1, 3: 2, 0: 3}
    x1_group, y1_group = copies.group(x1), copies.group(y1)
    ring_x1 = [
        Ring4(
            copies,
            x1_group,
            lambda off, h, k=k: wb.at[core, 2 * k, x_rows(off, h)],
            x1.at[k],
            at(dx=1),
            at(dx=-1),
        )
        for k in range(4)
    ]
    ring_y1 = [
        Ring4(
            copies,
            y1_group,
            lambda off, h, k=k: wb.at[core, 2 * order[off] + 1, x_rows(offsets[k], h)],
            y1.at[k],
            at(dy=1),
            at(dy=-1),
        )
        for k in range(4)
    ]
    ring_x2 = Ring4(
        copies,
        copies.group(x2),
        lambda off, h: wb.at[core, 2 * order[off], x_rows(0, h)],
        x2,
        at(dy=1),
        at(dy=-1),
    )
    ring_y2 = Ring4(
        copies,
        copies.group(y2),
        lambda off, h: wb.at[core, 7, x_rows(off, h)],
        y2,
        at(dx=1),
        at(dx=-1),
    )
    stage2 = (ring_x2, ring_y2)

    def pair_add(s):
        copies.wait(wd.at[s], pair + s)
        wb[core, s] = wb[core, s] + wd[s]
        if s % 2 == 0:
            ring_x1[s // 2].send2()
        elif s == 1:
            for ring in ring_y1:
                ring.send2()

    phase("add01")
    pair_add(0)
    pair_add(1)
    pl.semaphore_wait(know.at[0], 2)
    pl.semaphore_wait(know.at[3], 4)
    signal(know.at[4], at(dx=2))
    signal(know.at[4], at(dy=2))
    for d in (2, -2):
        signal(know.at[1], at(dz=d))
    phase("prod3")
    product(3)
    pair_send(3)
    phase("add23")
    pair_add(2)
    pair_add(3)
    phase("add45")
    pair_add(4)
    pair_add(5)
    phase("add67")
    pair_add(6)
    pair_add(7)

    def direct(k):
        for ring in (ring_x1[k], ring_y1[k]):
            ring.direct_plus()
            ring.direct_minus()

    def accumulate(k):
        for ring in (ring_x1[k], ring_y1[k]):
            ring.acc(0)
            ring.acc(1)

    direct(0)
    phase("bnpair")
    copies.wait(bnd, bn_pair)
    bnp[:, half] = bnp[:, half] + bnd[...]
    pl.semaphore_wait(know.at[4], 2)
    pl.semaphore_wait(know.at[1], 2)
    for d in (4, -4):
        signal(know.at[2], at(dz=d))

    def f_xy(dx, dy):
        start = mine + lax.rem(x + dx, NX) * F_X + lax.rem(y + dy, NY) * F_Y
        return pl.ds(mul(start, F_Y), F_Y)

    xy_group, xy = copies.group(bnx.at[1:16]), copies.arrivals()
    for dx, dy in plane:
        slot = bnx.at[4 * dx + dy]
        copies.start(bnp.at[:, f_xy(dx, dy)], slot, at(dx=dx, dy=dy), xy_group, xy)

    for k in range(4):
        phase(f"acc{k}")
        accumulate(k)
        if k < 3:
            direct(k + 1)

    phase("bnxy")
    copies.wait(bnx.at[1:16], xy)
    pl.semaphore_wait(know.at[2], 2)
    total = bnp[:, f_xy(0, 0)]
    for dx, dy in plane:
        total = total + bnx[4 * dx + dy]
    bnz[z] = total
    bz_group, bz = copies.group(bnz.at[0:15]), copies.arrivals()
    for d in far:
        copies.start(bnz.at[z], bnz.at[z], at(dz=d), bz_group, bz)

    def final(k):
        for h, v in enumerate(ring_x1[k].final()):
            wb[core, 2 * k, x_rows(0, h)] = v
        for h, v in enumerate(ring_y1[k].final()):
            wb[core, 7, x_rows(offsets[k], h)] = v

    phase("fin0")
    final(0)
    for ring in stage2:
        ring.send2()
    phase("fin1")
    final(1)
    for ring in stage2:
        ring.direct_plus()
    phase("fin2")
    final(2)
    for ring in stage2:
        ring.direct_minus()
    phase("accs2")
    for ring in stage2:
        ring.acc(0)
        ring.acc(1)
    phase("fin3")
    final(3)

    z_group, z_arrival = copies.group(zr.at[0:15]), copies.arrivals()

    def weight_z(colour):
        for h, v in enumerate(stage2[colour].final()):
            for i in range(2):
                zs[2 * colour + i, h * 32 : h * 32 + 32, :] = v[:, i * 128 : i * 128 + 128]
        for j in range(8):
            ll, hh = 2 * colour + j % 2, lax.rem(zh + offsets[j // 2], NZH)
            copy = copies.make(
                zs.at[ll, pl.ds(mul(hh * 16, 16), 16)],
                zr.at[z],
                (y * NZL + ll, (hh * NX + x) * 2 + core),
                z_group,
                z_arrival,
            )
            if j < 6:
                copy.start()
            else:
                pl.when(ll != zl)(copy.start)

    phase("wgtz0")
    weight_z(0)
    phase("wgtz1")
    weight_z(1)

    phase("bnz")
    copies.wait(bnz.at[0:15], bz)
    total = bnz[0]
    for i in range(1, NZ):
        total = total + bnz[i]
    own = bna.at[:, f_xy(0, 0)]
    own[...] = total * (1.0 / IMAGES)
    axy_group, axy = copies.group(bnz.at[0:15]), copies.arrivals()
    for dx, dy in plane:
        copies.start(own, own, at(dx=dx, dy=dy), axy_group, axy)
    zr[z] = zs[zl, pl.ds(mul(zh * 16, 16), 16)]

    phase("zwait")
    copies.wait(zr.at[0:15], z_arrival)
    result = zr[0]
    for i in range(1, NZ):
        result = result + zr[i]
    column = mul(zl // 2 * 1024 + y * W + lax.rem(zl, 2) * 128, 128)
    piece = wg.at[:, pl.ds(column, 128)]
    piece[...] = result * (1.0 / IMAGES)

    phase("ag")
    peers = [(2, 3), (2, 1), (2, 2), (1, 3), (3, 3), (1, 1), (3, 1), (1, 2), (3, 2)]
    peers += [(2, 0), (0, 3), (0, 1), (0, 2), (1, 0), (3, 0)]
    ag_group, ag = copies.group(zr.at[0:15]), copies.arrivals()
    for dy, dl in peers:
        device = (lax.rem(y + dy, NY) * NZL + lax.rem(zl + dl, NZL), zero)
        copies.start(piece, piece, device, ag_group, ag)

    phase("bngxy")
    copies.wait(bnz.at[0:15], axy)
    ap = copies.arrivals()
    whole_half = bna.at[:, half]
    copies.start(whole_half, whole_half, at(dc=1), copies.group(bnd), ap)
    phase("bngp")
    copies.wait(bnd, ap)
    loads["gain"].wait()

    def grads(i, carry):
        cols = pl.ds(mul(i * 512, 512), 512)
        g = up[:, cols].astype(jnp.float32)
        n = (pre[:, cols].astype(jnp.float32) - mean[:, cols]) * inv[:, cols]
        scale = gain[:, cols] * inv[:, cols]
        bias_grad, gain_grad = bna[0:1, cols], bna[1:2, cols]
        bias_o[:, cols] = bias_grad
        gain_o[:, cols] = gain_grad
        ig[:, cols] = (scale * (g - bias_grad - n * gain_grad)).astype(jnp.bfloat16)
        return carry

    phase("grads")
    lax.fori_loop(0, F // 512, grads, 0)
    phase("agwait")
    copies.wait(zr.at[0:15], ag)
    phase("drain")
    copies.drain()
    phase(None)
    assert (len(copies.sends), copies.n_recv) == (N_SEND, N_RECV), "semaphore counts"


N_SEND, N_RECV = 12, 45


def store(ig, gain, bias, wg, ig_o, gain_o, bias_o, wg_o, sem):
    pairs = ((ig, ig_o), (wg, wg_o), (gain, gain_o), (bias, bias_o))
    copies = [pltpu.make_async_copy(a, b, sem.at[i]) for i, (a, b) in enumerate(pairs)]
    for copy in copies:
        copy.start()
    for copy in copies:
        copy.wait()


def per_device(pre_norm, upstream, norm_gain, saved_mean, inv_std, features, out_grads):
    row = lambda v: v.reshape(1, F)
    f32, bf16 = jnp.float32, jnp.bfloat16
    vm = pltpu.VMEM
    dma = pltpu.SemaphoreType.DMA
    outs = (
        jax.ShapeDtypeStruct((16, F), bf16),
        jax.ShapeDtypeStruct((1, F), f32),
        jax.ShapeDtypeStruct((1, F), f32),
        jax.ShapeDtypeStruct((16, COUT), f32),
    )
    vectors = (row(norm_gain), row(saved_mean), row(inv_std))
    arrays = (pre_norm, upstream, *vectors, features, out_grads)
    results = pl.pallas_call(
        kernel,
        out_shape=outs,
        in_specs=[pl.BlockSpec(memory_space=pltpu.HBM)] * 7,
        out_specs=(pl.BlockSpec(memory_space=vm),) * 4,
        scratch_shapes=[
            vm((16, F), bf16), vm((16, F), bf16), vm((1, F), f32), vm((1, F), f32), vm((1, F), f32),
            vm((ROWS, CIN), bf16), vm((4, ROWS, 2 * W), bf16),
            vm((2, 8, 256, W), f32), vm((8, 256, W), f32),
            vm((4, 6, 32, W), f32), vm((4, 6, 32, W), f32), vm((6, 32, W), f32), vm((6, 32, W), f32),
            vm((NZL, 64, 128), f32), vm((NZ, 16, 128), f32),
            vm((2, F), f32), vm((2, F_CORE), f32), vm((16, 2, F_Y), f32),
            vm((NZ, 2, F_Y), f32), vm((2, F), f32),
            dma((14,)), dma((N_SEND,)), dma((N_RECV,)), pltpu.SemaphoreType.REGULAR((5,)),
        ],
        compiler_params=pltpu.CompilerParams(
            collective_id=0, has_side_effects=True, vmem_limit_bytes=32 * 1024 * 1024
        ),
        name="twins",
    )(*(pltpu.with_memory_space_constraint(v, pltpu.HBM) for v in arrays))
    ig, gain_grad, bias_grad, wg = pl.pallas_call(
        store,
        out_shape=outs,
        in_specs=[pl.BlockSpec(memory_space=pl.ANY)] * 4,
        out_specs=(pl.BlockSpec(memory_space=pltpu.HBM),) * 4,
        scratch_shapes=[dma((4,))],
        name="store",
    )(*(pltpu.with_memory_space_constraint(v, vm) for v in results))
    return ig, gain_grad.reshape(F), bias_grad.reshape(F), wg


def solution(mesh):
    split = P(("rep", "zero"), None)
    return jax.shard_map(
        per_device,
        mesh=mesh,
        in_specs=(split, split, P(), P(), P(), split, split),
        out_specs=(split, P(), P(), P("zero", None)),
        check_vma=False,
    )
```

time: 258 us -> 47.3 us (0.18)
  waiting for transfers between devices: 162 us -> 0 us
  blocking collectives: 46.8 us -> 0 us
  Pallas kernels: 0 us -> 46.5 us
  between operations: 15.5 us -> 0.64 us
  other arithmetic: 13.5 us -> 0 us
  local copies, waits for them, and re-layouts: 9.28 us -> 0 us
  starting transfers between devices: 6.71 us -> 0 us
  matrix products: 3.51 us -> 0 us
    all_gather x1 -> x0, waiting for transfers between devices: 63.9 us -> none  [gathered_total(): parts = lax.all_gather(x, axis)]
    reduce_scatter x2 -> x0, waiting for transfers between devices: 55.2 us -> none  [the longest x1 30.9 us: summed_rows(): return lax.psum_scatter(parts, chips, scatter_dimension=0, tiled=True)[0]]
    all_to_all x1 -> x0, blocking collectives: 46.8 us -> none  [sent_to_all(): return lax.all_to_all(copies, axis, split_axis=0, concat_axis=0, tiled=True)]
    pallas_call x0 -> x2, Pallas kernels: none -> 46.5 us  [the longest x1 45.7 us: per_device(): pl.pallas_call(kernel, out_shape=outs, in_specs=[pl.BlockSpec(memory_spac...]
    all_to_all x1 -> x0, waiting for transfers between devices: 42.7 us -> none  [sent_to_all(): return lax.all_to_all(copies, axis, split_axis=0, concat_axis=0, tiled=True)]
    reduce_sum x4 -> x0, other arithmetic: 8 us -> none  [the longest x2 3.89 us: taken_together(): return jnp.sum(everything, axis=0)]
    all_to_all x1 -> x0, starting transfers between devices: 6.58 us -> none  [sent_to_all(): return lax.all_to_all(copies, axis, split_axis=0, concat_axis=0, tiled=True)]
    broadcast_in_dim x2 -> x0, local copies, waits for them, and re-layouts: 3.73 us -> none  [sent_to_all(): copies = jnp.broadcast_to(x, (lax.axis_size(axis), *x.shape))]
  transfers between devices with their start and end apart: 4 -> 0, of which waited for: 4 -> 0; matrix products, arithmetic and copies ran while one was open for 5% -> 0% of each run, Pallas kernels for 0% -> 0%
where the time goes in v3:
time: 47.3 us; the launch traced here: 47.2 us
  Pallas kernels  46.5 us (98%)
  between operations  0.64 us (1%)
    pallas_call x1, Pallas kernels, per_device(): pl.pallas_call(kernel, out_shape=outs, in_specs=[pl.BlockSpec(memory_spac...  45.7 us

profile of v3, /device:TPU:4, one launch (start us, length us, event | category | flops | bytes accessed | tf_op | source)
XLA Modules:
  0.0 47.2 jit_solution(3711372126507830663)
XLA Ops:
  0.6 45.7 %twins.1 = (bf16[16,8192]{1,0:T(8,128)(2,1)S(1)}, f32[1,8192]{1,0:T(1,128)S(1)}, f32[1,8192]{1,0:T(1,128)S(1)}, f32[16,2048]{1,0:T(8,128)S(1)}) custom-call(bf16[16,8192]{1,0:T(8,128)(2,1)} %pre_h.1, bf16[16,8192]{1,0:T(8,128)(2,1)} %up_h.1, f32[1,8192]{1,0:T(1,128)} %bitcast.5, f32[1,8192]{1,0:T(1,128)} %bitcast.6, f32[1,8192]{1,0:T(1,128)} %bitcast.7, ...), custom_call_target="tpu_custom_call" | custom-call | tf_op jit(solution)/shard_map/twins/pallas_call | solution.py:477
  46.4 0.8 %store.1 = (bf16[16,8192]{1,0:T(8,128)(2,1)}, f32[1,8192]{1,0:T(1,128)}, f32[1,8192]{1,0:T(1,128)}, f32[16,2048]{1,0:T(8,128)}) custom-call(bf16[16,8192]{1,0:T(8,128)(2,1)S(1)} %get-tuple-element.12.ig, f32[1,8192]{1,0:T(1,128)S(1)} %get-tuple-element.13.gain, f32[1,8192]{1,0:T(1,128)S(1)} %get-tuple-element.14.bias, f32[16,2048]{1,0:T(8,128)S(1)} %get-tuple-element.15.wg), custom_call_target="tpu_custom_call" | custom-call | tf_op jit(solution)/shard_map/store/pallas_call | solution.py:497

commit v4 on v3

--- a/solution.py
+++ b/solution.py
@@ -71,40 +71,44 @@
 
 
 class Ring4:
-    def __init__(self, copies, group, src, bufs, plus, minus):
+    def __init__(self, copies, group, src, bufs, plus, minus, split=False):
         self.c, self.group, self.src, self.bufs = copies, group, src, bufs
         self.plus, self.minus = plus, minus
-        self.arrival = copies.arrivals(3)
+        self.arrival = copies.arrivals(3 if split else 2)
+        self.split = split
 
     def copy(self, ref, slot, device, arrival):
         self.c.start(ref, self.bufs.at[slot], device, self.group, self.arrival + arrival)
 
     def send2(self):
-        self.copy(self.src(2, 0), 0, self.plus, 0)
-        self.copy(self.src(2, 1), 1, self.minus, 1)
+        self.copy(self.src(2, 0), 0, self.plus, 1)
+        self.copy(self.src(2, 1), 1, self.minus, 2 if self.split else 1)
 
     def direct_plus(self):
-        self.copy(self.src(1, 1), 3, self.plus, 2)
+        self.copy(self.src(1, 1), 3, self.plus, 0)
 
     def direct_minus(self):
-        self.copy(self.src(3, 0), 2, self.minus, 2)
+        self.copy(self.src(3, 0), 2, self.minus, 0)
 
     def acc(self, half):
-        self.c.wait(self.bufs.at[half], self.arrival + half)
+        if self.split:
+            self.c.wait(self.bufs.at[half], self.arrival + 1 + half)
+        elif half == 0:
+            self.c.wait(self.bufs.at[0:2], self.arrival + 1)
         ref = self.src(1 if half == 0 else 3, half)
         ref[...] = ref[...] + self.bufs[half]
-        self.copy(ref, 4 + half, self.plus if half == 0 else self.minus, 2)
+        self.copy(ref, 4 + half, self.plus if half == 0 else self.minus, 0)
 
     def final(self):
-        self.c.wait(self.bufs.at[2:6], self.arrival + 2)
+        self.c.wait(self.bufs.at[2:6], self.arrival)
         return [self.src(0, h)[...] + self.bufs[2 + h] + self.bufs[4 + h] for h in range(2)]
 
 
 def kernel(
     pre_h, up_h, gain_h, mean_h, inv_h, feat_h, og_h,
     ig, gain_o, bias_o, wg,
-    pre, up, gain, mean, inv, feat, og,
-    wb, wd, x1, y1, x2, y2, zs, zr,
+    rows, vectors, feat, og,
+    wb, wd, rings, zs, zr,
     bnp, bnd, bnx, bnz, bna,
     local_sem, send_sem, recv_sem, know,
 ):
@@ -123,24 +127,31 @@
 
     phase = Phases()
     phase("start")
-    loads = {}
-
-    def load(name, src, dst):
-        loads[name] = pltpu.make_async_copy(src, dst, local_sem.at[len(loads)])
-        loads[name].start()
-
-    load("up", up_h, up)
-    load("pre", pre_h, pre)
-    load("mean", mean_h, mean)
-    load("inv", inv_h, inv)
-    load("feat", feat_h, feat)
     offsets = (2, 1, 3, 0)
+    pltpu.make_async_copy(feat_h, feat, local_sem.at[4]).start()
     for k in range(4):
         for colour in range(2):
             column = mul(colour * 1024 + lax.rem(y + offsets[k], NY) * W, W)
             dst = og.at[k, :, colour * W : colour * W + W]
-            load(("og", 2 * k + colour), og_h.at[:, pl.ds(column, W)], dst)
-    load("gain", gain_h, gain)
+            pltpu.make_async_copy(og_h.at[:, pl.ds(column, W)], dst, local_sem.at[k]).start()
+        if k == 1:
+            pltpu.make_async_copy(up_h, rows.at[0], local_sem.at[5]).start()
+            pltpu.make_async_copy(pre_h, rows.at[1], local_sem.at[5]).start()
+            for i, v in enumerate((mean_h, inv_h, gain_h)):
+                pltpu.make_async_copy(v, vectors.at[i], local_sem.at[6]).start()
+
+    def loaded(ref, i):
+        pltpu.make_async_remote_copy(
+            src_ref=ref,
+            dst_ref=ref,
+            send_sem=local_sem.at[i],
+            recv_sem=local_sem.at[i],
+            device_id=at(dc=1),
+            device_id_type=MESH,
+        ).wait_recv()
+
+    up, pre = rows.at[0], rows.at[1]
+    mean, inv, gain = vectors.at[0], vectors.at[1], vectors.at[2]
 
     def signal(sem, device):
         pl.semaphore_signal(sem, inc=1, device_id=device, device_id_type=MESH)
@@ -159,26 +170,11 @@
     other = (1 - core) * F_CORE
     half = pl.ds(mul(mine, F_CORE), F_CORE)
 
-    phase("bnload")
-    for name in ("up", "pre", "mean", "inv"):
-        loads[name].wait()
-
-    def sums(i, carry):
-        cols = pl.ds(mul(i * 512, 512), 512)
-        g = up[:, cols].astype(jnp.float32)
-        n = (pre[:, cols].astype(jnp.float32) - mean[:, cols]) * inv[:, cols]
-        bnp[0:1, cols] = jnp.sum(g, axis=0, keepdims=True)
-        bnp[1:2, cols] = jnp.sum(g * n, axis=0, keepdims=True)
-        return carry
-
-    phase("bnsum")
-    lax.fori_loop(0, F // 512, sums, 0)
     phase("featwait")
-    loads["feat"].wait()
+    loaded(feat, 4)
 
     def product(k):
-        loads[("og", 2 * k)].wait()
-        loads[("og", 2 * k + 1)].wait()
+        loaded(og.at[k], k)
         v = lax.dot_general(
             feat[...], og[k], (((0,), (0,)), ((), ())), preferred_element_type=jnp.float32
         )
@@ -208,28 +204,38 @@
     for d in (1, -1):
         signal(know.at[0], at(dz=d))
     pair_send(0)
+    phase("prod1")
+    product(1)
+    pair_send(1)
+    phase("bnload")
+    loaded(rows, 5)
+    loaded(vectors, 6)
+
+    def sums(i, carry):
+        cols = pl.ds(mul(i * 512, 512), 512)
+        g = up[:, cols].astype(jnp.float32)
+        n = (pre[:, cols].astype(jnp.float32) - mean[:, cols]) * inv[:, cols]
+        bnp[0:1, cols] = jnp.sum(g, axis=0, keepdims=True)
+        bnp[1:2, cols] = jnp.sum(g * n, axis=0, keepdims=True)
+        return carry
+
+    phase("bnsum")
+    lax.fori_loop(0, F // 512, sums, 0)
     bn_pair = copies.arrivals()
     copies.start(
         bnp.at[:, pl.ds(mul(other, F_CORE), F_CORE)], bnd, at(dc=1), copies.group(bnd), bn_pair
     )
-    phase("prod1")
-    product(1)
-    pair_send(1)
-    phase("prod2")
-    product(2)
-    pair_send(2)
-
     def x_rows(xx, h):
         return pl.ds(mul(lax.rem(x + xx, NX) * 64 + h * 32, 32), 32)
 
     order = {2: 0, 1: 1, 3: 2, 0: 3}
-    x1_group, y1_group = copies.group(x1), copies.group(y1)
+    ring_group = copies.group(rings)
     ring_x1 = [
         Ring4(
             copies,
-            x1_group,
+            ring_group,
             lambda off, h, k=k: wb.at[core, 2 * k, x_rows(off, h)],
-            x1.at[k],
+            rings.at[k],
             at(dx=1),
             at(dx=-1),
         )
@@ -238,9 +244,9 @@
     ring_y1 = [
         Ring4(
             copies,
-            y1_group,
+            ring_group,
             lambda off, h, k=k: wb.at[core, 2 * order[off] + 1, x_rows(offsets[k], h)],
-            y1.at[k],
+            rings.at[4 + k],
             at(dy=1),
             at(dy=-1),
         )
@@ -248,64 +254,71 @@
     ]
     ring_x2 = Ring4(
         copies,
-        copies.group(x2),
+        ring_group,
         lambda off, h: wb.at[core, 2 * order[off], x_rows(0, h)],
-        x2,
+        rings.at[8],
         at(dy=1),
         at(dy=-1),
+        split=True,
     )
     ring_y2 = Ring4(
         copies,
-        copies.group(y2),
+        ring_group,
         lambda off, h: wb.at[core, 7, x_rows(off, h)],
-        y2,
+        rings.at[9],
         at(dx=1),
         at(dx=-1),
+        split=True,
     )
     stage2 = (ring_x2, ring_y2)
 
     def pair_add(s):
         copies.wait(wd.at[s], pair + s)
         wb[core, s] = wb[core, s] + wd[s]
-        if s % 2 == 0:
-            ring_x1[s // 2].send2()
-        elif s == 1:
-            for ring in ring_y1:
-                ring.send2()
-
-    phase("add01")
+
+    def direct(ring):
+        ring.direct_plus()
+        ring.direct_minus()
+
+    def accumulate(ring):
+        ring.acc(0)
+        ring.acc(1)
+
+    def final_x(k):
+        for h, v in enumerate(ring_x1[k].final()):
+            wb[core, 2 * k, x_rows(0, h)] = v
+
+    def final_y(k):
+        for h, v in enumerate(ring_y1[k].final()):
+            wb[core, 7, x_rows(offsets[k], h)] = v
+
+    phase("add0")
     pair_add(0)
-    pair_add(1)
+    ring_x1[0].send2()
+    direct(ring_x1[0])
     pl.semaphore_wait(know.at[0], 2)
     pl.semaphore_wait(know.at[3], 4)
     signal(know.at[4], at(dx=2))
     signal(know.at[4], at(dy=2))
     for d in (2, -2):
         signal(know.at[1], at(dz=d))
+    phase("prod2")
+    product(2)
+    pair_send(2)
+    phase("add12")
+    pair_add(1)
+    ring_y1[0].send2()
+    ring_y1[1].send2()
+    pair_add(2)
+    ring_x1[1].send2()
     phase("prod3")
     product(3)
     pair_send(3)
-    phase("add23")
-    pair_add(2)
+    phase("add3")
     pair_add(3)
-    phase("add45")
-    pair_add(4)
-    pair_add(5)
-    phase("add67")
-    pair_add(6)
-    pair_add(7)
-
-    def direct(k):
-        for ring in (ring_x1[k], ring_y1[k]):
-            ring.direct_plus()
-            ring.direct_minus()
-
-    def accumulate(k):
-        for ring in (ring_x1[k], ring_y1[k]):
-            ring.acc(0)
-            ring.acc(1)
-
-    direct(0)
+    ring_y1[2].send2()
+    ring_y1[3].send2()
+    ring_y1[0].direct_plus()
     phase("bnpair")
     copies.wait(bnd, bn_pair)
     bnp[:, half] = bnp[:, half] + bnd[...]
@@ -323,47 +336,52 @@
         slot = bnx.at[4 * dx + dy]
         copies.start(bnp.at[:, f_xy(dx, dy)], slot, at(dx=dx, dy=dy), xy_group, xy)
 
-    for k in range(4):
-        phase(f"acc{k}")
-        accumulate(k)
-        if k < 3:
-            direct(k + 1)
-
-    phase("bnxy")
-    copies.wait(bnx.at[1:16], xy)
-    pl.semaphore_wait(know.at[2], 2)
-    total = bnp[:, f_xy(0, 0)]
-    for dx, dy in plane:
-        total = total + bnx[4 * dx + dy]
-    bnz[z] = total
-    bz_group, bz = copies.group(bnz.at[0:15]), copies.arrivals()
-    for d in far:
-        copies.start(bnz.at[z], bnz.at[z], at(dz=d), bz_group, bz)
-
-    def final(k):
-        for h, v in enumerate(ring_x1[k].final()):
-            wb[core, 2 * k, x_rows(0, h)] = v
-        for h, v in enumerate(ring_y1[k].final()):
-            wb[core, 7, x_rows(offsets[k], h)] = v
-
-    phase("fin0")
-    final(0)
-    for ring in stage2:
-        ring.send2()
-    phase("fin1")
-    final(1)
-    for ring in stage2:
-        ring.direct_plus()
-    phase("fin2")
-    final(2)
-    for ring in stage2:
-        ring.direct_minus()
-    phase("accs2")
-    for ring in stage2:
-        ring.acc(0)
-        ring.acc(1)
-    phase("fin3")
-    final(3)
+    phase("add45")
+    pair_add(4)
+    ring_x1[2].send2()
+    pair_add(5)
+    ring_y1[0].direct_minus()
+    phase("acc0")
+    accumulate(ring_x1[0])
+    phase("add67")
+    pair_add(6)
+    ring_x1[3].send2()
+    direct(ring_x1[1])
+    pair_add(7)
+    phase("acc0y")
+    accumulate(ring_y1[0])
+    direct(ring_y1[1])
+    def bn_z():
+        copies.wait(bnx.at[1:16], xy)
+        pl.semaphore_wait(know.at[2], 2)
+        total = bnp[:, f_xy(0, 0)]
+        for dx, dy in plane:
+            total = total + bnx[4 * dx + dy]
+        bnz[z] = total
+        bz_group, bz = copies.group(bnz.at[0:15]), copies.arrivals()
+        for d in far:
+            copies.start(bnz.at[z], bnz.at[z], at(dz=d), bz_group, bz)
+        return bz
+
+    first, second = {"X": ring_x1, "Y": ring_y1}, {"X": ring_x2, "Y": ring_y2}
+    finals = {"X": final_x, "Y": final_y}
+
+    bz = None
+    for step in " ".join(ORDER).split():
+        phase(step)
+        kind, c, k = step[0], step[1:2], int(step[2:3] or 0)
+        if kind == "a":
+            accumulate(first[c][k])
+        elif kind == "d":
+            direct(first[c][k])
+        elif kind == "s":
+            second[c].acc(k)
+        elif kind == "f":
+            finals[c](k)
+            if k < 3:
+                (second[c].send2, second[c].direct_plus, second[c].direct_minus)[k]()
+        else:
+            bz = bn_z()
 
     z_group, z_arrival = copies.group(zr.at[0:15]), copies.arrivals()
 
@@ -397,9 +415,12 @@
         total = total + bnz[i]
     own = bna.at[:, f_xy(0, 0)]
     own[...] = total * (1.0 / IMAGES)
-    axy_group, axy = copies.group(bnz.at[0:15]), copies.arrivals()
-    for dx, dy in plane:
-        copies.start(own, own, at(dx=dx, dy=dy), axy_group, axy)
+    others = bna.at[:, 0 : 31 * F_Y]
+    axy_group, axy = copies.group(others), copies.arrivals()
+    for dx, dy in plane + [(0, 0)]:
+        for dc in (1, 0):
+            if dx or dy or dc:
+                copies.start(own, own, at(dx=dx, dy=dy, dc=dc), axy_group, axy)
     zr[z] = zs[zl, pl.ds(mul(zh * 16, 16), 16)]
 
     phase("zwait")
@@ -420,13 +441,7 @@
         copies.start(piece, piece, device, ag_group, ag)
 
     phase("bngxy")
-    copies.wait(bnz.at[0:15], axy)
-    ap = copies.arrivals()
-    whole_half = bna.at[:, half]
-    copies.start(whole_half, whole_half, at(dc=1), copies.group(bnd), ap)
-    phase("bngp")
-    copies.wait(bnd, ap)
-    loads["gain"].wait()
+    copies.wait(others, axy)
 
     def grads(i, carry):
         cols = pl.ds(mul(i * 512, 512), 512)
@@ -449,7 +464,11 @@
     assert (len(copies.sends), copies.n_recv) == (N_SEND, N_RECV), "semaphore counts"
 
 
-N_SEND, N_RECV = 12, 45
+N_SEND, N_RECV = 8, 36
+ORDER = (
+    "aX1 dX2 aY1 aX2", "fX0 dY2 aY2 dX3", "fY0 fX1 dY3 aX3", "aY3 fY1 b",
+    "sX0 sY0 fX2 sX1", "fY2 sY1 fX3 fY3",
+)
 
 
 def store(ig, gain, bias, wg, ig_o, gain_o, bias_o, wg_o, sem):
@@ -480,14 +499,13 @@
         in_specs=[pl.BlockSpec(memory_space=pltpu.HBM)] * 7,
         out_specs=(pl.BlockSpec(memory_space=vm),) * 4,
         scratch_shapes=[
-            vm((16, F), bf16), vm((16, F), bf16), vm((1, F), f32), vm((1, F), f32), vm((1, F), f32),
-            vm((ROWS, CIN), bf16), vm((4, ROWS, 2 * W), bf16),
+            vm((2, 16, F), bf16), vm((3, 1, F), f32), vm((ROWS, CIN), bf16), vm((4, ROWS, 2 * W), bf16),
             vm((2, 8, 256, W), f32), vm((8, 256, W), f32),
-            vm((4, 6, 32, W), f32), vm((4, 6, 32, W), f32), vm((6, 32, W), f32), vm((6, 32, W), f32),
+            vm((10, 6, 32, W), f32),
             vm((NZL, 64, 128), f32), vm((NZ, 16, 128), f32),
             vm((2, F), f32), vm((2, F_CORE), f32), vm((16, 2, F_Y), f32),
             vm((NZ, 2, F_Y), f32), vm((2, F), f32),
-            dma((14,)), dma((N_SEND,)), dma((N_RECV,)), pltpu.SemaphoreType.REGULAR((5,)),
+            dma((7,)), dma((N_SEND,)), dma((N_RECV,)), pltpu.SemaphoreType.REGULAR((5,)),
         ],
         compiler_params=pltpu.CompilerParams(
             collective_id=0, has_side_effects=True, vmem_limit_bytes=32 * 1024 * 1024

time: 47.3 us -> 45.8 us (0.968)
  the two profiles are of different devices: /device:TPU:4 before, /device:TPU:2 now
where the time goes in v4:
time: 45.8 us; the launch traced here: 45.7 us
  Pallas kernels  45.1 us (98%)
  between operations  0.64 us (1%)
    pallas_call x1, Pallas kernels, per_device(): pl.pallas_call(kernel, out_shape=outs, in_specs=[pl.BlockSpec(memory_spac...  44.3 us

profile of v4, /device:TPU:2, one launch (start us, length us, event | category | flops | bytes accessed | tf_op | source)
XLA Modules:
  0.0 45.7 jit_solution(17735698441144134607)
XLA Ops:
  0.6 44.3 %twins.1 = (bf16[16,8192]{1,0:T(8,128)(2,1)S(1)}, f32[1,8192]{1,0:T(1,128)S(1)}, f32[1,8192]{1,0:T(1,128)S(1)}, f32[16,2048]{1,0:T(8,128)S(1)}) custom-call(bf16[16,8192]{1,0:T(8,128)(2,1)} %pre_h.1, bf16[16,8192]{1,0:T(8,128)(2,1)} %up_h.1, f32[1,8192]{1,0:T(1,128)} %bitcast.5, f32[1,8192]{1,0:T(1,128)} %bitcast.6, f32[1,8192]{1,0:T(1,128)} %bitcast.7, ...), custom_call_target="tpu_custom_call" | custom-call | tf_op jit(solution)/shard_map/twins/pallas_call | solution.py:496
  44.9 0.8 %store.1 = (bf16[16,8192]{1,0:T(8,128)(2,1)}, f32[1,8192]{1,0:T(1,128)}, f32[1,8192]{1,0:T(1,128)}, f32[16,2048]{1,0:T(8,128)}) custom-call(bf16[16,8192]{1,0:T(8,128)(2,1)S(1)} %get-tuple-element.12.ig, f32[1,8192]{1,0:T(1,128)S(1)} %get-tuple-element.13.gain, f32[1,8192]{1,0:T(1,128)S(1)} %get-tuple-element.14.bias, f32[16,2048]{1,0:T(8,128)S(1)} %get-tuple-element.15.wg), custom_call_target="tpu_custom_call" | custom-call | tf_op jit(solution)/shard_map/store/pallas_call | solution.py:515

commit v5 on v4

--- a/solution.py
+++ b/solution.py
@@ -108,7 +108,7 @@
     pre_h, up_h, gain_h, mean_h, inv_h, feat_h, og_h,
     ig, gain_o, bias_o, wg,
     rows, vectors, feat, og,
-    wb, wd, rings, zs, zr,
+    wb, wd, rings, half_rings, zx, zy, own_sums, zs, zr,
     bnp, bnd, bnx, bnz, bna,
     local_sem, send_sem, recv_sem, know,
 ):
@@ -127,11 +127,13 @@
 
     phase = Phases()
     phase("start")
-    offsets = (2, 1, 3, 0)
+    offsets, own_early = (2, 1, 3, 0), (2, 1, 0, 3)
+    slot_x = (0, 2, 6, 4)
     pltpu.make_async_copy(feat_h, feat, local_sem.at[4]).start()
     for k in range(4):
         for colour in range(2):
-            column = mul(colour * 1024 + lax.rem(y + offsets[k], NY) * W, W)
+            off = (offsets, own_early)[colour == 0][k]
+            column = mul(colour * 1024 + lax.rem(y + off, NY) * W, W)
             dst = og.at[k, :, colour * W : colour * W + W]
             pltpu.make_async_copy(og_h.at[:, pl.ds(column, W)], dst, local_sem.at[k]).start()
         if k == 1:
@@ -229,13 +231,23 @@
         return pl.ds(mul(lax.rem(x + xx, NX) * 64 + h * 32, 32), 32)
 
     order = {2: 0, 1: 1, 3: 2, 0: 3}
-    ring_group = copies.group(rings)
+    ring_group, half_group = copies.group(rings), copies.group(half_rings)
+    parity = lax.rem(zl, 2)
+    kept = pl.ds(mul(parity * 128, 128), 128)
+    given = pl.ds(mul((1 - parity) * 128, 128), 128)
+
+    def bufs(k, colour):
+        return half_rings.at[colour] if k == 3 else rings.at[3 * colour + k]
+
+    def columns(k):
+        return kept if k == 3 else slice(None)
+
     ring_x1 = [
         Ring4(
             copies,
-            ring_group,
-            lambda off, h, k=k: wb.at[core, 2 * k, x_rows(off, h)],
-            rings.at[k],
+            half_group if k == 3 else ring_group,
+            lambda off, h, k=k: wb.at[core, slot_x[k], x_rows(off, h), columns(k)],
+            bufs(k, 0),
             at(dx=1),
             at(dx=-1),
         )
@@ -244,9 +256,11 @@
     ring_y1 = [
         Ring4(
             copies,
-            ring_group,
-            lambda off, h, k=k: wb.at[core, 2 * order[off] + 1, x_rows(offsets[k], h)],
-            rings.at[4 + k],
+            half_group if k == 3 else ring_group,
+            lambda off, h, k=k: wb.at[
+                core, 2 * order[off] + 1, x_rows(offsets[k], h), columns(k)
+            ],
+            bufs(k, 1),
             at(dy=1),
             at(dy=-1),
         )
@@ -255,8 +269,10 @@
     ring_x2 = Ring4(
         copies,
         ring_group,
-        lambda off, h: wb.at[core, 2 * order[off], x_rows(0, h)],
-        rings.at[8],
+        lambda off, h: (
+            wb.at[core, slot_x[order[off]], x_rows(0, h)] if off else own_sums.at[0, h]
+        ),
+        rings.at[6],
         at(dy=1),
         at(dy=-1),
         split=True,
@@ -264,12 +280,38 @@
     ring_y2 = Ring4(
         copies,
         ring_group,
-        lambda off, h: wb.at[core, 7, x_rows(off, h)],
-        rings.at[9],
+        lambda off, h: wb.at[core, 7, x_rows(off, h)] if off else own_sums.at[1, h],
+        rings.at[7],
         at(dx=1),
         at(dx=-1),
         split=True,
     )
+    zx_group, zy_group = copies.group(zx), copies.group(zy)
+    zx_arrival, zy_arrival = copies.arrivals(), copies.arrivals(2)
+
+    def z_exchange_x():
+        for i in range(2):
+            src = wb.at[core, slot_x[3], 128 * i : 128 * i + 128, given]
+            copies.start(src, zx.at[i], at(dz=1 - 2 * i), zx_group, zx_arrival)
+
+    def z_exchange_y(k):
+        for i in range(2):
+            src = wb.at[core, 2 * k + 1, x_rows(0, i), given]
+            copies.start(src, zy.at[k, i], at(dz=1 - 2 * i), zy_group, zy_arrival + min(k, 1))
+
+    def z_add_x():
+        copies.wait(zx, zx_arrival)
+        for i in range(2):
+            ref = wb.at[core, slot_x[3], 128 * i : 128 * i + 128, kept]
+            ref[...] = ref[...] + zx[i]
+
+    def z_add_y(first, n):
+        copies.wait(zy.at[first : first + n], zy_arrival + min(first, 1))
+        for k in range(first, first + n):
+            for i in range(2):
+                ref = wb.at[core, 2 * k + 1, x_rows(0, i), kept]
+                ref[...] = ref[...] + zy[k, i]
+
     stage2 = (ring_x2, ring_y2)
 
     def pair_add(s):
@@ -286,11 +328,17 @@
 
     def final_x(k):
         for h, v in enumerate(ring_x1[k].final()):
-            wb[core, 2 * k, x_rows(0, h)] = v
+            if k == 3:
+                own_sums[0, h, :, kept] = v
+            else:
+                wb[core, slot_x[k], x_rows(0, h)] = v
 
     def final_y(k):
         for h, v in enumerate(ring_y1[k].final()):
-            wb[core, 7, x_rows(offsets[k], h)] = v
+            if k == 3:
+                own_sums[1, h, :, kept] = v
+            else:
+                wb[core, 7, x_rows(offsets[k], h)] = v
 
     phase("add0")
     pair_add(0)
@@ -307,6 +355,7 @@
     pair_send(2)
     phase("add12")
     pair_add(1)
+    z_exchange_y(0)
     ring_y1[0].send2()
     ring_y1[1].send2()
     pair_add(2)
@@ -316,8 +365,8 @@
     pair_send(3)
     phase("add3")
     pair_add(3)
+    z_exchange_y(1)
     ring_y1[2].send2()
-    ring_y1[3].send2()
     ring_y1[0].direct_plus()
     phase("bnpair")
     copies.wait(bnd, bn_pair)
@@ -338,16 +387,19 @@
 
     phase("add45")
     pair_add(4)
-    ring_x1[2].send2()
+    z_exchange_x()
     pair_add(5)
+    z_exchange_y(2)
     ring_y1[0].direct_minus()
     phase("acc0")
     accumulate(ring_x1[0])
     phase("add67")
     pair_add(6)
-    ring_x1[3].send2()
+    ring_x1[2].send2()
     direct(ring_x1[1])
     pair_add(7)
+    z_exchange_y(3)
+    own_sums[...] = jnp.zeros_like(own_sums)
     phase("acc0y")
     accumulate(ring_y1[0])
     direct(ring_y1[1])
@@ -370,6 +422,13 @@
     for step in " ".join(ORDER).split():
         phase(step)
         kind, c, k = step[0], step[1:2], int(step[2:3] or 0)
+        if kind == "z":
+            z_add_x() if c == "X" else z_add_y(0, 1)
+            first[c][3].send2()
+            continue
+        if kind == "y":
+            z_add_y(1, 3)
+            continue
         if kind == "a":
             accumulate(first[c][k])
         elif kind == "d":
@@ -464,10 +523,10 @@
     assert (len(copies.sends), copies.n_recv) == (N_SEND, N_RECV), "semaphore counts"
 
 
-N_SEND, N_RECV = 8, 36
+N_SEND, N_RECV = 11, 39
 ORDER = (
-    "aX1 dX2 aY1 aX2", "fX0 dY2 aY2 dX3", "fY0 fX1 dY3 aX3", "aY3 fY1 b",
-    "sX0 sY0 fX2 sX1", "fY2 sY1 fX3 fY3",
+    "aX1 dX2 aY1 aX2", "fX0 zY dY2 zX", "aY2 fY0 y b", "fX1 dX3 dY3 fY1",
+    "aX3 aY3 sX0 sY0", "fX2 sX1 fY2 sY1", "fX3 fY3",
 )
 
 
@@ -501,7 +560,8 @@
         scratch_shapes=[
             vm((2, 16, F), bf16), vm((3, 1, F), f32), vm((ROWS, CIN), bf16), vm((4, ROWS, 2 * W), bf16),
             vm((2, 8, 256, W), f32), vm((8, 256, W), f32),
-            vm((10, 6, 32, W), f32),
+            vm((8, 6, 32, W), f32), vm((2, 6, 32, W // 2), f32),
+            vm((2, 128, W // 2), f32), vm((4, 2, 32, W // 2), f32), vm((2, 2, 32, W), f32),
             vm((NZL, 64, 128), f32), vm((NZ, 16, 128), f32),
             vm((2, F), f32), vm((2, F_CORE), f32), vm((16, 2, F_Y), f32),
             vm((NZ, 2, F_Y), f32), vm((2, F), f32),

time: 45.8 us -> 45.6 us (level)
  no operation moved by 1% of the time
where the time goes in v5:
time: 45.6 us; the launch traced here: 45.5 us
  Pallas kernels  44.8 us (98%)
  between operations  0.64 us (1%)
    pallas_call x1, Pallas kernels, per_device(): pl.pallas_call(kernel, out_shape=outs, in_specs=[pl.BlockSpec(memory_spac...  44 us

profile of v5, /device:TPU:2, one launch (start us, length us, event | category | flops | bytes accessed | tf_op | source)
XLA Modules:
  0.0 45.5 jit_solution(3204810364215599484)
XLA Ops:
  0.6 44.0 %twins.1 = (bf16[16,8192]{1,0:T(8,128)(2,1)S(1)}, f32[1,8192]{1,0:T(1,128)S(1)}, f32[1,8192]{1,0:T(1,128)S(1)}, f32[16,2048]{1,0:T(8,128)S(1)}) custom-call(bf16[16,8192]{1,0:T(8,128)(2,1)} %pre_h.1, bf16[16,8192]{1,0:T(8,128)(2,1)} %up_h.1, f32[1,8192]{1,0:T(1,128)} %bitcast.5, f32[1,8192]{1,0:T(1,128)} %bitcast.6, f32[1,8192]{1,0:T(1,128)} %bitcast.7, ...), custom_call_target="tpu_custom_call" | custom-call | tf_op jit(solution)/shard_map/twins/pallas_call | solution.py:555
  44.7 0.8 %store.1 = (bf16[16,8192]{1,0:T(8,128)(2,1)}, f32[1,8192]{1,0:T(1,128)}, f32[1,8192]{1,0:T(1,128)}, f32[16,2048]{1,0:T(8,128)}) custom-call(bf16[16,8192]{1,0:T(8,128)(2,1)S(1)} %get-tuple-element.12.ig, f32[1,8192]{1,0:T(1,128)S(1)} %get-tuple-element.13.gain, f32[1,8192]{1,0:T(1,128)S(1)} %get-tuple-element.14.bias, f32[16,2048]{1,0:T(8,128)S(1)} %get-tuple-element.15.wg), custom_call_target="tpu_custom_call" | custom-call | tf_op jit(solution)/shard_map/store/pallas_call | solution.py:575

commit v6 on v5

--- a/solution.py
+++ b/solution.py
@@ -492,12 +492,17 @@
     piece[...] = result * (1.0 / IMAGES)
 
     phase("ag")
-    peers = [(2, 3), (2, 1), (2, 2), (1, 3), (3, 3), (1, 1), (3, 1), (1, 2), (3, 2)]
-    peers += [(2, 0), (0, 3), (0, 1), (0, 2), (1, 0), (3, 0)]
     ag_group, ag = copies.group(zr.at[0:15]), copies.arrivals()
-    for dy, dl in peers:
-        device = (lax.rem(y + dy, NY) * NZL + lax.rem(zl + dl, NZL), zero)
-        copies.start(piece, piece, device, ag_group, ag)
+    far_first = [(2, 0), (1, 0), (3, 0), (2, 1), (0, 0), (1, 1), (3, 1), (2, 2), (0, 1)]
+    far_first += [(1, 2), (3, 2), (2, 3), (0, 2), (1, 3), (3, 3), (0, 3)]
+    for dy, i in far_first:
+        to = i + (1 - zl // 2) * (3 - 2 * i)
+        device = (lax.rem(y + dy, NY) * NZL + to, zero)
+        copy = copies.make(piece, piece, device, ag_group, ag)
+        if dy:
+            copy.start()
+        else:
+            pl.when(to != zl)(copy.start)
 
     phase("bngxy")
     copies.wait(others, axy)

time: 45.6 us -> 45.4 us (level)
  the two profiles are of different devices: /device:TPU:2 before, /device:TPU:8 now
where the time goes in v6:
time: 45.4 us; the launch traced here: 45.2 us
  Pallas kernels  44.6 us (98%)
  between operations  0.64 us (1%)
    pallas_call x1, Pallas kernels, per_device(): pl.pallas_call(kernel, out_shape=outs, in_specs=[pl.BlockSpec(memory_spac...  43.8 us

profile of v6, /device:TPU:8, one launch (start us, length us, event | category | flops | bytes accessed | tf_op | source)
XLA Modules:
  0.0 45.2 jit_solution(15653629801408006525)
XLA Ops:
  0.6 43.8 %twins.1 = (bf16[16,8192]{1,0:T(8,128)(2,1)S(1)}, f32[1,8192]{1,0:T(1,128)S(1)}, f32[1,8192]{1,0:T(1,128)S(1)}, f32[16,2048]{1,0:T(8,128)S(1)}) custom-call(bf16[16,8192]{1,0:T(8,128)(2,1)} %pre_h.1, bf16[16,8192]{1,0:T(8,128)(2,1)} %up_h.1, f32[1,8192]{1,0:T(1,128)} %bitcast.5, f32[1,8192]{1,0:T(1,128)} %bitcast.6, f32[1,8192]{1,0:T(1,128)} %bitcast.7, ...), custom_call_target="tpu_custom_call" | custom-call | tf_op jit(solution)/shard_map/twins/pallas_call | solution.py:560
  44.4 0.8 %store.1 = (bf16[16,8192]{1,0:T(8,128)(2,1)}, f32[1,8192]{1,0:T(1,128)}, f32[1,8192]{1,0:T(1,128)}, f32[16,2048]{1,0:T(8,128)}) custom-call(bf16[16,8192]{1,0:T(8,128)(2,1)S(1)} %get-tuple-element.12.ig, f32[1,8192]{1,0:T(1,128)S(1)} %get-tuple-element.13.gain, f32[1,8192]{1,0:T(1,128)S(1)} %get-tuple-element.14.bias, f32[16,2048]{1,0:T(8,128)S(1)} %get-tuple-element.15.wg), custom_call_target="tpu_custom_call" | custom-call | tf_op jit(solution)/shard_map/store/pallas_call | solution.py:580
